TPU v7x, 256 devices: a whole 4x4x8 slice. The times are simulated.
256 devices in a mesh: grp: 8 (over z), sp: 32 (over y, x, core).
Axes of the slice: x: 4, y: 4, z: 8, core: 2. Of those that a mesh axis runs over, the one named last changes fastest.
Arguments:
- tokens: bfloat16 [16384, 2880], P(('grp', 'sp')), may hold values from -36 to 36
- query_weight: bfloat16 [2880, 2048], P(None, 'sp'), may hold values from -0.109375 to 0.109375
- key_value_weight: bfloat16 [2880, 1024], replicated, may hold values from -0.109375 to 0.109375
- block_places: int32 [32], replicated, may hold values from 0 to 31, each once
- sinks: float32 [32], replicated, may hold values from -1 to 5
Outputs:
- attended: bfloat16 [16384, 2048], P(('grp', 'sp'))
Inputs may be any that keep to these rules, and one draw needn't show every extreme that they name: `block_places`: every sequence block appears once.
All inputs are finite; a program needn't handle non-finite values.
Results may differ from a plain program's by a relative error of at most 0.008.
The roundings to bfloat16 on the way count: a program that leaves them out, or rounds other values in their place, can miss the bound.
Values may be sent and summed in bfloat16 or wider, within the bound.
A program may use at most 128 MiB of HBM per device.

v0:
```python
import jax
import jax.numpy as jnp
from jax import lax
from jax.sharding import PartitionSpec as P

QUERY_HEADS = 32
HEAD_SIZE = 64
BPG = 4


rope_base = 150000.0
neg_large = -1e30


def joined_along(pieces, dim):
    pieces = jnp.moveaxis(pieces, 0, dim)
    shape = pieces.shape
    return pieces.reshape(*shape[:dim], shape[dim] * shape[dim + 1], *shape[dim + 2 :])


def piecewise(value, axis, dim, apply, out_dim):
    size, span = (lax.axis_size(axis), value.shape[dim])
    count = 2 if span % 2 == 0 else 1
    finished, length = ([], span // count)
    for k in range(count):
        share = lax.slice_in_dim(value, k * length, (k + 1) * length, axis=dim)
        starts = jnp.arange(size) * span + k * length
        finished.append(jax.vmap(apply)(lax.all_gather(share, axis), starts))
    return joined_along(jnp.concatenate(finished, axis=out_dim + 1), out_dim)


def rotate(vectors, angles):
    middle = vectors.shape[-1] // 2
    first_half = vectors[..., :middle]
    second_half = vectors[..., middle:]
    cosine = jnp.cos(angles)
    sine_part = jnp.sin(angles)
    return jnp.concatenate(
        [
            first_half * cosine - second_half * sine_part,
            second_half * cosine + first_half * sine_part,
        ],
        axis=-1,
    )


def locate(stored, block_rows, block_places):
    blocks = stored // block_rows
    table = jnp.arange(block_places.shape[0], dtype=jnp.int32)
    onehot = (blocks[:, None] == table[None, :]).astype(jnp.int32)
    return jnp.sum(onehot * block_places[None, :], axis=1) * block_rows + stored % block_rows


def prepare(projected, own_places, query_cols, kv_cols, head_count):
    row_count = projected.shape[0]
    inverse = rope_base ** (-(jnp.arange(HEAD_SIZE // 2, dtype=jnp.float32) * 2.0) / HEAD_SIZE)
    angles = own_places.astype(jnp.float32)[:, None, None] * inverse[None, None, :]
    queries = rotate(
        projected[:, :query_cols].reshape(row_count, query_cols // HEAD_SIZE, HEAD_SIZE), angles
    ).astype(jnp.bfloat16)
    rotated_keys = rotate(
        projected[:, query_cols : query_cols + kv_cols].reshape(row_count, head_count, HEAD_SIZE),
        angles,
    )
    key_value_pair = jnp.concatenate(
        [rotated_keys.reshape(row_count, kv_cols), projected[:, query_cols + kv_cols :]], axis=1
    ).astype(jnp.bfloat16)
    return (queries, key_value_pair)


def attend(state, queries, query_places, key_value_pair, key_places, head_count):
    maxima, totals, mixture = state
    key_count = key_value_pair.shape[0]
    column_half = key_value_pair.shape[1] // 2
    key_part = key_value_pair[:, :column_half].reshape(key_count, head_count, HEAD_SIZE)
    value_part = key_value_pair[:, column_half:].reshape(key_count, head_count, HEAD_SIZE)
    scores = jnp.einsum(
        "qhgd,khd->hgqk", queries, key_part, preferred_element_type=jnp.float32
    ) * HEAD_SIZE ** (-0.5)
    allowed = key_places[None, :] <= query_places[:, None]
    scores = jnp.where(allowed, scores, neg_large)
    updated = jnp.maximum(maxima, jnp.max(scores, axis=-1))
    weights = jnp.where(allowed, jnp.exp(scores - updated[..., None]), 0.0)
    factor = jnp.exp(maxima - updated)
    totals = totals * factor + jnp.sum(weights, axis=-1)
    mixture = mixture * factor[..., None] + jnp.einsum(
        "hgqk,khd->hgqd",
        weights.astype(jnp.bfloat16),
        value_part,
        preferred_element_type=jnp.float32,
    )
    return (updated, totals, mixture)


def per_device(tokens, query_weight, key_value_weight, block_places, sinks):
    sp_count = lax.axis_size("sp")
    local_rows = tokens.shape[0]
    group_rows = local_rows * sp_count
    block_rows = group_rows // BPG
    kv_total = key_value_weight.shape[1] // (2 * HEAD_SIZE)
    sp_place = lax.axis_index("sp")
    grp_place = lax.axis_index("grp")
    query_cols = query_weight.shape[1]
    query_heads = query_cols // HEAD_SIZE
    head_count = max(kv_total // sp_count, 1)
    kv_cols = head_count * HEAD_SIZE
    first_head = sp_place * query_heads // (QUERY_HEADS // kv_total)
    key_weight = lax.dynamic_slice_in_dim(key_value_weight, first_head * HEAD_SIZE, kv_cols, 1)
    value_weight = lax.dynamic_slice_in_dim(
        key_value_weight, kv_total * HEAD_SIZE + first_head * HEAD_SIZE, kv_cols, 1
    )
    joined = jnp.concatenate([query_weight, key_weight, value_weight], axis=1)

    def project(piece, start):
        return jnp.dot(piece, joined, preferred_element_type=jnp.float32)

    projected = piecewise(tokens, "sp", 0, project, 0)
    query_local = jnp.arange(group_rows, dtype=jnp.int32)
    head_first = sp_place * query_heads
    own_places = locate(grp_place * group_rows + query_local, block_rows, block_places)
    queries, key_value_pair = prepare(projected, own_places, query_cols, kv_cols, head_count)
    query_sharing = query_heads // head_count
    head_sinks = lax.dynamic_slice_in_dim(sinks, head_first, query_heads, 0).reshape(
        head_count, query_sharing
    )
    sink_rows = jnp.broadcast_to(head_sinks[:, :, None], (head_count, query_sharing, group_rows))
    query_block4 = queries.reshape(group_rows, head_count, query_sharing, HEAD_SIZE)
    initial = (
        sink_rows,
        jnp.ones((head_count, query_sharing, group_rows), jnp.float32),
        jnp.zeros((head_count, query_sharing, group_rows, HEAD_SIZE), jnp.float32),
    )
    piece = lax.all_gather(key_value_pair, "grp", axis=0, tiled=True)
    step_rows = min(piece.shape[0], group_rows)
    turns = piece.shape[0] // step_rows

    def visit(turn, inner):
        offset = turn * step_rows
        piece_rows = lax.dynamic_slice_in_dim(piece, offset, step_rows, 0)
        position = offset + jnp.arange(step_rows, dtype=jnp.int32)
        stored = position // group_rows * group_rows + position % group_rows
        key_places = locate(stored, block_rows, block_places)
        return attend(inner, query_block4, own_places, piece_rows, key_places, head_count)

    maxima, totals, mixture = lax.fori_loop(0, turns, visit, initial)
    normed = jnp.transpose(mixture, (2, 0, 1, 3)) / jnp.transpose(totals, (2, 0, 1))[..., None]
    attended = normed.reshape(group_rows, query_cols).astype(jnp.bfloat16)
    return lax.all_to_all(attended, "sp", split_axis=0, concat_axis=1, tiled=True)


def solution(mesh):
    in_specs = (P(("grp", "sp"), None), P(None, "sp"), P(), P(), P())
    out_specs = P(("grp", "sp"), None)
    return jax.shard_map(
        per_device, mesh=mesh, in_specs=in_specs, out_specs=out_specs, check_vma=False
    )
```

profile of v0, /device:TPU:1, one launch (start us, length us, event | category | flops | bytes accessed | tf_op | source)
XLA Modules:
  0.0 353.2 jit_solution(3869679549317436455)
XLA Ops:
  6.5 1.8 fusion.61
  8.4 0.7 all-gather.10.cloned.1.call-update
  9.2 1.8 constant_dynamic-slice_fusion.1
  11.8 55.8 %all-gather.8.cloned.1.call-done = bf16[1024,2880]{1,0:T(8,128)(2,1)} async-done(((bf16[32,2880]{1,0:T(8,128)(2,1)}), bf16[1024,2880]{1,0:T(8,128)(2,1)}) %all-gather.8.cloned.1.call-update) | async-done | bytes 5898256 | tf_op jit(solution)/shard_map/all_gather | solution.py:28
  67.6 4.5 %convolution_bitcast_fusion.1 = f32[32,32,192]{2,1,0:T(8,128)S(1)} fusion(bf16[32,32,2880]{2,1,0:T(8,128)(2,1)} %bitcast.94, bf16[2880,64]{0,1:T(8,128)(2,1)S(1)} %copy.44, bf16[2880,64]{0,1:T(8,128)(2,1)S(1)} %copy.43, bf16[2880,64]{0,1:T(8,128)(2,1)S(1)} %copy-done.2), kind=kOutput, calls=%fused_computation.49 | convolution fusion | flops 1135779840 | bytes 7790592 | tf_op jit(solution)/shard_map/vmap()/dot_general | solution.py:115
  72.1 50.5 %all-gather.10.cloned.1.call-done = bf16[1024,2880]{1,0:T(8,128)(2,1)} async-done(((bf16[32,2880]{1,0:T(8,128)(2,1)}), bf16[1024,2880]{1,0:T(8,128)(2,1)}) %all-gather.10.cloned.1.call-update) | async-done | bytes 5898256 | tf_op jit(solution)/shard_map/all_gather | solution.py:28
  122.6 4.5 %convolution_bitcast_fusion = f32[32,32,192]{2,1,0:T(8,128)S(1)} fusion(bf16[32,32,2880]{2,1,0:T(8,128)(2,1)} %bitcast.95, bf16[2880,64]{0,1:T(8,128)(2,1)S(1)} %copy.44, bf16[2880,64]{0,1:T(8,128)(2,1)S(1)} %copy.43, bf16[2880,64]{0,1:T(8,128)(2,1)S(1)} %copy-done.2), kind=kOutput, calls=%fused_computation.48 | convolution fusion | flops 1135779840 | bytes 7790592 | tf_op jit(solution)/shard_map/vmap()/dot_general | solution.py:115
  128.6 1.2 fusion.49
  129.9 0.8 pad_maximum_fusion.1
  130.7 0.6 dynamic_slice.20
  131.3 52.6 %all-gather.6.cloned.1.call-done = bf16[16384,128]{0,1:T(8,128)(2,1)} async-done(((bf16[2048,128]{0,1:T(8,128)(2,1)}), bf16[16384,128]{0,1:T(8,128)(2,1)}) %all-gather.6.cloned.1.call-update) | async-done | bytes 4194320 | tf_op jit(solution)/shard_map/all_gather | solution.py:133
  183.9 0.6 broadcast_in_dim.68
  184.5 141.5 %while.21 = (s32[]{:T(128)}, f32[1,1,2048]{2,1,0:T(1,128)S(1)}, f32[1,1,2048]{2,1,0:T(1,128)S(1)}, f32[1,1,2048,64]{2,3,1,0:T(8,128)S(1)}, s32[32]{0:T(128)S(1)}...) while((s32[]{:T(128)}, f32[1,1,2048]{2,1,0:T(1,128)S(1)}, ...), condition=%wide.region_5.6_spmd.clone, body=%wide.region_1.5_spmd.clone.sunk | while | flops 1141592064 | bytes 119497064 | solution.py:145
  184.7 3.6 %fusion.74 = (f32[2048]{0:T(1024)S(1)}, f32[2048,2048]{1,0:T(8,128)S(1)}) fusion(s32[2048]{0:T(1024)S(1)} %get-tuple-element.427, s32[2048]{0:T(1024)S(1)} %fusion.73, bf16[2048,1,1,64]{0,3,2,1:T(8,128)(2,1)S(1)} %get-tuple-element.429, bf16[16384,128]{0,1:T(8,128)(2,1)} %get-tuple-element.428, s32[]{:T(128)S(6)} %select_n.248), kind=kOutput, calls=%fused_computation.2.clone.1 | convolution fusion | flops 553646080 | bytes 17326084 | tf_op jit(solution)/shard_map/while/body/eval_jaxpr/qhgd,khd->hgqk/dot_general | solution.py:77
  188.3 5.3 %fusion.75 = f32[2048]{0:T(1024)S(1)} fusion(f32[2048,2048]{1,0:T(8,128)S(1)} %get-tuple-element.393, f32[2048]{0:T(1024)S(1)} %bitcast.86, s32[2048]{0:T(1024)S(1)} %get-tuple-element.427, s32[2048]{0:T(1024)S(1)} %fusion.73), kind=kLoop, calls=%fused_computation.4.clone.1 | loop fusion | flops 25163776 | bytes 16809984 | tf_op jit(solution)/shard_map/while/body/eval_jaxpr/reduce_sum | solution.py:85
  193.6 0.4 copy-done
  194.1 8.1 %fusion.77 = f32[1,1,2048,64]{2,3,1,0:T(8,128)S(1)} fusion(f32[2048,2048]{1,0:T(8,128)} %copy-done, f32[2048]{0:T(1024)S(1)} %bitcast.87, s32[2048]{0:T(1024)S(1)} %get-tuple-element.427, s32[2048]{0:T(1024)S(1)} %fusion.73, f32[1,1,2048,64]{2,3,1,0:T(8,128)S(1)} %get-tuple-element.412, bf16[16384,128]{0,1:T(8,128)(2,1)} %get-tuple-element.428, ...), kind=kOutput, calls=%fused_computation.8.clone.1 | convolution fusion | flops 562429952 | bytes 18120712 | tf_op jit(solution)/shard_map/while/body/eval_jaxpr/hgqk,khd->hgqd/dot_general | solution.py:86
  202.4 3.6 %fusion.74 = (f32[2048]{0:T(1024)S(1)}, f32[2048,2048]{1,0:T(8,128)S(1)}) fusion(s32[2048]{0:T(1024)S(1)} %get-tuple-element.427, s32[2048]{0:T(1024)S(1)} %fusion.73, bf16[2048,1,1,64]{0,3,2,1:T(8,128)(2,1)S(1)} %get-tuple-element.429, bf16[16384,128]{0,1:T(8,128)(2,1)} %get-tuple-element.428, s32[]{:T(128)S(6)} %select_n.248), kind=kOutput, calls=%fused_computation.2.clone.1 | convolution fusion | flops 553646080 | bytes 17326084 | tf_op jit(solution)/shard_map/while/body/eval_jaxpr/qhgd,khd->hgqk/dot_general | solution.py:77
  206.0 5.3 %fusion.75 = f32[2048]{0:T(1024)S(1)} fusion(f32[2048,2048]{1,0:T(8,128)S(1)} %get-tuple-element.393, f32[2048]{0:T(1024)S(1)} %bitcast.86, s32[2048]{0:T(1024)S(1)} %get-tuple-element.427, s32[2048]{0:T(1024)S(1)} %fusion.73), kind=kLoop, calls=%fused_computation.4.clone.1 | loop fusion | flops 25163776 | bytes 16809984 | tf_op jit(solution)/shard_map/while/body/eval_jaxpr/reduce_sum | solution.py:85
  211.3 0.4 copy-done
  211.8 8.1 %fusion.77 = f32[1,1,2048,64]{2,3,1,0:T(8,128)S(1)} fusion(f32[2048,2048]{1,0:T(8,128)} %copy-done, f32[2048]{0:T(1024)S(1)} %bitcast.87, s32[2048]{0:T(1024)S(1)} %get-tuple-element.427, s32[2048]{0:T(1024)S(1)} %fusion.73, f32[1,1,2048,64]{2,3,1,0:T(8,128)S(1)} %get-tuple-element.412, bf16[16384,128]{0,1:T(8,128)(2,1)} %get-tuple-element.428, ...), kind=kOutput, calls=%fused_computation.8.clone.1 | convolution fusion | flops 562429952 | bytes 18120712 | tf_op jit(solution)/shard_map/while/body/eval_jaxpr/hgqk,khd->hgqd/dot_general | solution.py:86
  220.1 3.6 %fusion.74 = (f32[2048]{0:T(1024)S(1)}, f32[2048,2048]{1,0:T(8,128)S(1)}) fusion(s32[2048]{0:T(1024)S(1)} %get-tuple-element.427, s32[2048]{0:T(1024)S(1)} %fusion.73, bf16[2048,1,1,64]{0,3,2,1:T(8,128)(2,1)S(1)} %get-tuple-element.429, bf16[16384,128]{0,1:T(8,128)(2,1)} %get-tuple-element.428, s32[]{:T(128)S(6)} %select_n.248), kind=kOutput, calls=%fused_computation.2.clone.1 | convolution fusion | flops 553646080 | bytes 17326084 | tf_op jit(solution)/shard_map/while/body/eval_jaxpr/qhgd,khd->hgqk/dot_general | solution.py:77
  223.7 5.3 %fusion.75 = f32[2048]{0:T(1024)S(1)} fusion(f32[2048,2048]{1,0:T(8,128)S(1)} %get-tuple-element.393, f32[2048]{0:T(1024)S(1)} %bitcast.86, s32[2048]{0:T(1024)S(1)} %get-tuple-element.427, s32[2048]{0:T(1024)S(1)} %fusion.73), kind=kLoop, calls=%fused_computation.4.clone.1 | loop fusion | flops 25163776 | bytes 16809984 | tf_op jit(solution)/shard_map/while/body/eval_jaxpr/reduce_sum | solution.py:85
  229.0 0.4 copy-done
  229.5 8.1 %fusion.77 = f32[1,1,2048,64]{2,3,1,0:T(8,128)S(1)} fusion(f32[2048,2048]{1,0:T(8,128)} %copy-done, f32[2048]{0:T(1024)S(1)} %bitcast.87, s32[2048]{0:T(1024)S(1)} %get-tuple-element.427, s32[2048]{0:T(1024)S(1)} %fusion.73, f32[1,1,2048,64]{2,3,1,0:T(8,128)S(1)} %get-tuple-element.412, bf16[16384,128]{0,1:T(8,128)(2,1)} %get-tuple-element.428, ...), kind=kOutput, calls=%fused_computation.8.clone.1 | convolution fusion | flops 562429952 | bytes 18120712 | tf_op jit(solution)/shard_map/while/body/eval_jaxpr/hgqk,khd->hgqd/dot_general | solution.py:86
  237.8 3.6 %fusion.74 = (f32[2048]{0:T(1024)S(1)}, f32[2048,2048]{1,0:T(8,128)S(1)}) fusion(s32[2048]{0:T(1024)S(1)} %get-tuple-element.427, s32[2048]{0:T(1024)S(1)} %fusion.73, bf16[2048,1,1,64]{0,3,2,1:T(8,128)(2,1)S(1)} %get-tuple-element.429, bf16[16384,128]{0,1:T(8,128)(2,1)} %get-tuple-element.428, s32[]{:T(128)S(6)} %select_n.248), kind=kOutput, calls=%fused_computation.2.clone.1 | convolution fusion | flops 553646080 | bytes 17326084 | tf_op jit(solution)/shard_map/while/body/eval_jaxpr/qhgd,khd->hgqk/dot_general | solution.py:77
  241.4 5.3 %fusion.75 = f32[2048]{0:T(1024)S(1)} fusion(f32[2048,2048]{1,0:T(8,128)S(1)} %get-tuple-element.393, f32[2048]{0:T(1024)S(1)} %bitcast.86, s32[2048]{0:T(1024)S(1)} %get-tuple-element.427, s32[2048]{0:T(1024)S(1)} %fusion.73), kind=kLoop, calls=%fused_computation.4.clone.1 | loop fusion | flops 25163776 | bytes 16809984 | tf_op jit(solution)/shard_map/while/body/eval_jaxpr/reduce_sum | solution.py:85
  246.7 0.4 copy-done
  247.1 8.1 %fusion.77 = f32[1,1,2048,64]{2,3,1,0:T(8,128)S(1)} fusion(f32[2048,2048]{1,0:T(8,128)} %copy-done, f32[2048]{0:T(1024)S(1)} %bitcast.87, s32[2048]{0:T(1024)S(1)} %get-tuple-element.427, s32[2048]{0:T(1024)S(1)} %fusion.73, f32[1,1,2048,64]{2,3,1,0:T(8,128)S(1)} %get-tuple-element.412, bf16[16384,128]{0,1:T(8,128)(2,1)} %get-tuple-element.428, ...), kind=kOutput, calls=%fused_computation.8.clone.1 | convolution fusion | flops 562429952 | bytes 18120712 | tf_op jit(solution)/shard_map/while/body/eval_jaxpr/hgqk,khd->hgqd/dot_general | solution.py:86
  255.5 3.6 %fusion.74 = (f32[2048]{0:T(1024)S(1)}, f32[2048,2048]{1,0:T(8,128)S(1)}) fusion(s32[2048]{0:T(1024)S(1)} %get-tuple-element.427, s32[2048]{0:T(1024)S(1)} %fusion.73, bf16[2048,1,1,64]{0,3,2,1:T(8,128)(2,1)S(1)} %get-tuple-element.429, bf16[16384,128]{0,1:T(8,128)(2,1)} %get-tuple-element.428, s32[]{:T(128)S(6)} %select_n.248), kind=kOutput, calls=%fused_computation.2.clone.1 | convolution fusion | flops 553646080 | bytes 17326084 | tf_op jit(solution)/shard_map/while/body/eval_jaxpr/qhgd,khd->hgqk/dot_general | solution.py:77
  259.1 5.3 %fusion.75 = f32[2048]{0:T(1024)S(1)} fusion(f32[2048,2048]{1,0:T(8,128)S(1)} %get-tuple-element.393, f32[2048]{0:T(1024)S(1)} %bitcast.86, s32[2048]{0:T(1024)S(1)} %get-tuple-element.427, s32[2048]{0:T(1024)S(1)} %fusion.73), kind=kLoop, calls=%fused_computation.4.clone.1 | loop fusion | flops 25163776 | bytes 16809984 | tf_op jit(solution)/shard_map/while/body/eval_jaxpr/reduce_sum | solution.py:85
  264.4 0.4 copy-done
  264.8 8.1 %fusion.77 = f32[1,1,2048,64]{2,3,1,0:T(8,128)S(1)} fusion(f32[2048,2048]{1,0:T(8,128)} %copy-done, f32[2048]{0:T(1024)S(1)} %bitcast.87, s32[2048]{0:T(1024)S(1)} %get-tuple-element.427, s32[2048]{0:T(1024)S(1)} %fusion.73, f32[1,1,2048,64]{2,3,1,0:T(8,128)S(1)} %get-tuple-element.412, bf16[16384,128]{0,1:T(8,128)(2,1)} %get-tuple-element.428, ...), kind=kOutput, calls=%fused_computation.8.clone.1 | convolution fusion | flops 562429952 | bytes 18120712 | tf_op jit(solution)/shard_map/while/body/eval_jaxpr/hgqk,khd->hgqd/dot_general | solution.py:86
  273.2 3.6 %fusion.74 = (f32[2048]{0:T(1024)S(1)}, f32[2048,2048]{1,0:T(8,128)S(1)}) fusion(s32[2048]{0:T(1024)S(1)} %get-tuple-element.427, s32[2048]{0:T(1024)S(1)} %fusion.73, bf16[2048,1,1,64]{0,3,2,1:T(8,128)(2,1)S(1)} %get-tuple-element.429, bf16[16384,128]{0,1:T(8,128)(2,1)} %get-tuple-element.428, s32[]{:T(128)S(6)} %select_n.248), kind=kOutput, calls=%fused_computation.2.clone.1 | convolution fusion | flops 553646080 | bytes 17326084 | tf_op jit(solution)/shard_map/while/body/eval_jaxpr/qhgd,khd->hgqk/dot_general | solution.py:77
  276.8 5.3 %fusion.75 = f32[2048]{0:T(1024)S(1)} fusion(f32[2048,2048]{1,0:T(8,128)S(1)} %get-tuple-element.393, f32[2048]{0:T(1024)S(1)} %bitcast.86, s32[2048]{0:T(1024)S(1)} %get-tuple-element.427, s32[2048]{0:T(1024)S(1)} %fusion.73), kind=kLoop, calls=%fused_computation.4.clone.1 | loop fusion | flops 25163776 | bytes 16809984 | tf_op jit(solution)/shard_map/while/body/eval_jaxpr/reduce_sum | solution.py:85
  282.1 0.4 copy-done
  282.5 8.1 %fusion.77 = f32[1,1,2048,64]{2,3,1,0:T(8,128)S(1)} fusion(f32[2048,2048]{1,0:T(8,128)} %copy-done, f32[2048]{0:T(1024)S(1)} %bitcast.87, s32[2048]{0:T(1024)S(1)} %get-tuple-element.427, s32[2048]{0:T(1024)S(1)} %fusion.73, f32[1,1,2048,64]{2,3,1,0:T(8,128)S(1)} %get-tuple-element.412, bf16[16384,128]{0,1:T(8,128)(2,1)} %get-tuple-element.428, ...), kind=kOutput, calls=%fused_computation.8.clone.1 | convolution fusion | flops 562429952 | bytes 18120712 | tf_op jit(solution)/shard_map/while/body/eval_jaxpr/hgqk,khd->hgqd/dot_general | solution.py:86
  290.9 3.6 %fusion.74 = (f32[2048]{0:T(1024)S(1)}, f32[2048,2048]{1,0:T(8,128)S(1)}) fusion(s32[2048]{0:T(1024)S(1)} %get-tuple-element.427, s32[2048]{0:T(1024)S(1)} %fusion.73, bf16[2048,1,1,64]{0,3,2,1:T(8,128)(2,1)S(1)} %get-tuple-element.429, bf16[16384,128]{0,1:T(8,128)(2,1)} %get-tuple-element.428, s32[]{:T(128)S(6)} %select_n.248), kind=kOutput, calls=%fused_computation.2.clone.1 | convolution fusion | flops 553646080 | bytes 17326084 | tf_op jit(solution)/shard_map/while/body/eval_jaxpr/qhgd,khd->hgqk/dot_general | solution.py:77
  294.5 5.3 %fusion.75 = f32[2048]{0:T(1024)S(1)} fusion(f32[2048,2048]{1,0:T(8,128)S(1)} %get-tuple-element.393, f32[2048]{0:T(1024)S(1)} %bitcast.86, s32[2048]{0:T(1024)S(1)} %get-tuple-element.427, s32[2048]{0:T(1024)S(1)} %fusion.73), kind=kLoop, calls=%fused_computation.4.clone.1 | loop fusion | flops 25163776 | bytes 16809984 | tf_op jit(solution)/shard_map/while/body/eval_jaxpr/reduce_sum | solution.py:85
  299.8 0.4 copy-done
  300.2 8.1 %fusion.77 = f32[1,1,2048,64]{2,3,1,0:T(8,128)S(1)} fusion(f32[2048,2048]{1,0:T(8,128)} %copy-done, f32[2048]{0:T(1024)S(1)} %bitcast.87, s32[2048]{0:T(1024)S(1)} %get-tuple-element.427, s32[2048]{0:T(1024)S(1)} %fusion.73, f32[1,1,2048,64]{2,3,1,0:T(8,128)S(1)} %get-tuple-element.412, bf16[16384,128]{0,1:T(8,128)(2,1)} %get-tuple-element.428, ...), kind=kOutput, calls=%fused_computation.8.clone.1 | convolution fusion | flops 562429952 | bytes 18120712 | tf_op jit(solution)/shard_map/while/body/eval_jaxpr/hgqk,khd->hgqd/dot_general | solution.py:86
  308.6 3.6 %fusion.74 = (f32[2048]{0:T(1024)S(1)}, f32[2048,2048]{1,0:T(8,128)S(1)}) fusion(s32[2048]{0:T(1024)S(1)} %get-tuple-element.427, s32[2048]{0:T(1024)S(1)} %fusion.73, bf16[2048,1,1,64]{0,3,2,1:T(8,128)(2,1)S(1)} %get-tuple-element.429, bf16[16384,128]{0,1:T(8,128)(2,1)} %get-tuple-element.428, s32[]{:T(128)S(6)} %select_n.248), kind=kOutput, calls=%fused_computation.2.clone.1 | convolution fusion | flops 553646080 | bytes 17326084 | tf_op jit(solution)/shard_map/while/body/eval_jaxpr/qhgd,khd->hgqk/dot_general | solution.py:77
  312.2 5.3 %fusion.75 = f32[2048]{0:T(1024)S(1)} fusion(f32[2048,2048]{1,0:T(8,128)S(1)} %get-tuple-element.393, f32[2048]{0:T(1024)S(1)} %bitcast.86, s32[2048]{0:T(1024)S(1)} %get-tuple-element.427, s32[2048]{0:T(1024)S(1)} %fusion.73), kind=kLoop, calls=%fused_computation.4.clone.1 | loop fusion | flops 25163776 | bytes 16809984 | tf_op jit(solution)/shard_map/while/body/eval_jaxpr/reduce_sum | solution.py:85
  317.9 8.1 %fusion.77 = f32[1,1,2048,64]{2,3,1,0:T(8,128)S(1)} fusion(f32[2048,2048]{1,0:T(8,128)} %copy-done, f32[2048]{0:T(1024)S(1)} %bitcast.87, s32[2048]{0:T(1024)S(1)} %get-tuple-element.427, s32[2048]{0:T(1024)S(1)} %fusion.73, f32[1,1,2048,64]{2,3,1,0:T(8,128)S(1)} %get-tuple-element.412, bf16[16384,128]{0,1:T(8,128)(2,1)} %get-tuple-element.428, ...), kind=kOutput, calls=%fused_computation.8.clone.1 | convolution fusion | flops 562429952 | bytes 18120712 | tf_op jit(solution)/shard_map/while/body/eval_jaxpr/hgqk,khd->hgqd/dot_general | solution.py:86
  326.4 0.5 broadcast.645
  326.9 0.7 reduce.17
  328.4 16.4 %all_to_all.16 = bf16[32,2,2048]{2,1,0:T(2,128)(2,1)S(1)} all-to-all(bf16[32,2,2048]{2,1,0:T(2,128)(2,1)S(1)} %reshape.437), channel_id=1, replica_groups=mesh['grp'=8,'sp'=32] {'sp'}, dimensions={0} | all-to-all | bytes 524288 | tf_op jit(solution)/shard_map/all_to_all | solution.py:148
  345.5 1.2 all_to_all.14
  (90 shorter events, 6.2 us)
Async XLA Ops:
  6.5 5.1 %copy-start.1 = (s32[32]{0:T(128)S(1)}, s32[32]{0:T(128)}, u32[]{:S(2)}) copy-start(s32[32]{0:T(128)} %param.10) | copy-start | bytes 388
  6.5 61.1 %copy-start.2 = (bf16[2880,64]{0,1:T(8,128)(2,1)S(1)}, bf16[2880,64]{0,1:T(8,128)(2,1)}, u32[]{:S(2)}) copy-start(bf16[2880,64]{0,1:T(8,128)(2,1)} %param.8) | copy-start | bytes 1105924
  6.5 61.1 %all-gather.8.cloned.1.call-start = ((), (), s32[]{:S(2)}) async-start(), calls=%async_computation.2 | async-start | bytes 6217728 | tf_op jit(solution)/shard_map/all_gather | solution.py:28
  8.4 114.2 %all-gather.10.cloned.1.call-start = ((), (), s32[]{:S(2)}) async-start(), calls=%async_computation.3 | async-start | bytes 6217728 | tf_op jit(solution)/shard_map/all_gather | solution.py:28
  9.1 174.8 %all-gather.6.cloned.1.call-start = ((), (), s32[]{:S(2)}) async-start(), calls=%async_computation.1 | async-start | bytes 4718592 | tf_op jit(solution)/shard_map/all_gather | solution.py:133
  127.3 3.4 copy-start.3
  188.3 5.7 %copy-start = (f32[2048,2048]{1,0:T(8,128)}, f32[2048,2048]{1,0:T(8,128)S(1)}, u32[]{:S(2)}) copy-start(f32[2048,2048]{1,0:T(8,128)S(1)} %get-tuple-element.393) | copy-start | bytes 50331652 | tf_op jit(solution)/shard_map/while
  206.0 5.7 %copy-start = (f32[2048,2048]{1,0:T(8,128)}, f32[2048,2048]{1,0:T(8,128)S(1)}, u32[]{:S(2)}) copy-start(f32[2048,2048]{1,0:T(8,128)S(1)} %get-tuple-element.393) | copy-start | bytes 50331652 | tf_op jit(solution)/shard_map/while
  223.7 5.7 %copy-start = (f32[2048,2048]{1,0:T(8,128)}, f32[2048,2048]{1,0:T(8,128)S(1)}, u32[]{:S(2)}) copy-start(f32[2048,2048]{1,0:T(8,128)S(1)} %get-tuple-element.393) | copy-start | bytes 50331652 | tf_op jit(solution)/shard_map/while
  241.4 5.7 %copy-start = (f32[2048,2048]{1,0:T(8,128)}, f32[2048,2048]{1,0:T(8,128)S(1)}, u32[]{:S(2)}) copy-start(f32[2048,2048]{1,0:T(8,128)S(1)} %get-tuple-element.393) | copy-start | bytes 50331652 | tf_op jit(solution)/shard_map/while
  259.1 5.7 %copy-start = (f32[2048,2048]{1,0:T(8,128)}, f32[2048,2048]{1,0:T(8,128)S(1)}, u32[]{:S(2)}) copy-start(f32[2048,2048]{1,0:T(8,128)S(1)} %get-tuple-element.393) | copy-start | bytes 50331652 | tf_op jit(solution)/shard_map/while
  276.8 5.7 %copy-start = (f32[2048,2048]{1,0:T(8,128)}, f32[2048,2048]{1,0:T(8,128)S(1)}, u32[]{:S(2)}) copy-start(f32[2048,2048]{1,0:T(8,128)S(1)} %get-tuple-element.393) | copy-start | bytes 50331652 | tf_op jit(solution)/shard_map/while
  294.5 5.7 %copy-start = (f32[2048,2048]{1,0:T(8,128)}, f32[2048,2048]{1,0:T(8,128)S(1)}, u32[]{:S(2)}) copy-start(f32[2048,2048]{1,0:T(8,128)S(1)} %get-tuple-element.393) | copy-start | bytes 50331652 | tf_op jit(solution)/shard_map/while
  312.2 5.7 %copy-start = (f32[2048,2048]{1,0:T(8,128)}, f32[2048,2048]{1,0:T(8,128)S(1)}, u32[]{:S(2)}) copy-start(f32[2048,2048]{1,0:T(8,128)S(1)} %get-tuple-element.393) | copy-start | bytes 50331652 | tf_op jit(solution)/shard_map/while
Sparse Core Ops, SparseCore 0:
  9.9 57.7 all-gather.7
  70.2 52.4 all-gather.9
  130.8 53.0 all-gather.5
where the time goes:
time: 354 us; the launch traced here: 353 us
  waiting for transfers between devices  160 us (45%)
  matrix products  103 us (29%)
  other arithmetic  47.6 us (13%)
  blocking collectives  16.4 us (5%)
  between operations  13.3 us (4%)
  local copies, waits for them, and re-layouts  12.9 us (4%)
    all_gather x2, waiting for transfers between devices, piecewise(): finished.append(jax.vmap(apply)(lax.all_gather(share, axis), starts))  106 us
    dot_general x8, matrix products, attend(): jnp.einsum('hgqk,khd->hgqd', weights.astype(jnp.bfloat16), value_part, pr...  65 us
    all_gather x1, waiting for transfers between devices, per_device(): piece = lax.all_gather(key_value_pair, 'grp', axis=0, tiled=True)  52.6 us
    reduce_sum x8, other arithmetic, attend(): totals = totals * factor + jnp.sum(weights, axis=-1)  42.5 us
    dot_general x8, matrix products, attend(): jnp.einsum('qhgd,khd->hgqk', queries, key_part, preferred_element_type=jn...  28.7 us
    all_to_all x1, blocking collectives, per_device(): lax.all_to_all(attended, 'sp', split_axis=0, concat_axis=1, tiled=True)  16.4 us
    dot_general x2, matrix products, project(): return jnp.dot(piece, joined, preferred_element_type=jnp.float32)  9.01 us
  transfers between devices with their start and end apart: 3, of which 3 were waited for; matrix products, arithmetic and copies ran while one was open for 2% of the time, Pallas kernels for 0%

commit v1 on v0

v1 whole, which is shorter than its diff:
```python
import math

import jax
import jax.numpy as jnp
import numpy as np
from jax import lax
from jax.experimental import pallas as pl
from jax.experimental.pallas import tpu as pltpu
from jax.sharding import PartitionSpec as P

MESH = pl.DeviceIdType.MESH
BF16, F32, I32 = jnp.bfloat16, jnp.float32, jnp.int32
WIDTH = 2880
HEAD = 64
BLK = 512
NBLK = 32
SCALE_LOG2 = HEAD**-0.5 * math.log2(math.e)
NEG = -1e30
VMEM = pl.BlockSpec(memory_space=pltpu.VMEM)
HBM = pl.BlockSpec(memory_space=pltpu.HBM)
SMEM = pl.BlockSpec(memory_space=pltpu.SMEM)
INVERSE = (150000.0 ** (-(np.arange(32, dtype=np.float64) * 2.0) / HEAD)).astype(np.float32)


def place():
    z = lax.axis_index("grp")
    s = lax.axis_index("sp")
    return z, s // 8, (s // 2) % 4, s % 2


def dev(z, y, x, c):
    return (z, (y * 4 + x) * 2 + c)


def dot(a, b, ca, cb):
    return lax.dot_general(a, b, (((ca,), (cb,)), ((), ())), preferred_element_type=F32)


def barrier_with(peers):
    sem = pltpu.get_barrier_semaphore()
    for peer in peers:
        pl.semaphore_signal(sem, inc=1, device_id=peer, device_id_type=MESH)
    pl.semaphore_wait(sem, len(peers))


def kv_kernel(places, inv_ref, tok_ref, wk_ref, wv_ref, wq_ref, kvp_ref, wqt_ref, cos_s, sin_s):
    z, y, x, c = place()
    lane = lax.broadcasted_iota(I32, (64, 128), 1)

    @pl.when(pl.program_id(0) == 0)
    def _():
        base = places[z * 4 + y] * BLK + (x * 2 + c) * 64
        pos = (base + lax.broadcasted_iota(I32, (64, 128), 0)).astype(F32)
        angle = pos * inv_ref[...]
        cos_s[...] = jnp.cos(angle)
        sin_s[...] = jnp.where(lane % 64 < 32, -1.0, 1.0) * jnp.sin(angle)
        eye = (
            lax.broadcasted_iota(I32, (64, 64), 0) == lax.broadcasted_iota(I32, (64, 64), 1)
        ).astype(BF16)
        wqt_ref[...] = dot(eye, wq_ref[...], 1, 1).astype(BF16)

    k = jnp.dot(tok_ref[...], wk_ref[...], preferred_element_type=F32)
    v = jnp.dot(tok_ref[...], wv_ref[...], preferred_element_type=F32)
    swapped = jnp.where(lane % 64 < 32, pltpu.roll(k, 96, 1), pltpu.roll(k, 32, 1))
    k = k * cos_s[...] + swapped * sin_s[...]
    kvp_ref[0] = jnp.where(lane < 64, k, pltpu.roll(v, 64, 1)).astype(BF16)
    kvp_ref[1] = jnp.where(lane < 64, pltpu.roll(k, 64, 1), v).astype(BF16)


def kv_project(places, tokens, kvw, wq):
    inv = jnp.asarray(np.tile(INVERSE, 4)[None, :])
    return pl.pallas_call(
        kv_kernel,
        grid=(4,),
        in_specs=[
            SMEM,
            pl.BlockSpec((1, 128), lambda n: (0, 0)),
            pl.BlockSpec((64, WIDTH), lambda n: (0, 0)),
            pl.BlockSpec((WIDTH, 128), lambda n: (0, n)),
            pl.BlockSpec((WIDTH, 128), lambda n: (0, 4 + n)),
            pl.BlockSpec((WIDTH, 64), lambda n: (0, 0)),
        ],
        out_specs=[
            pl.BlockSpec((2, 64, 128), lambda n: (n, 0, 0)),
            pl.BlockSpec((64, WIDTH), lambda n: (0, 0)),
        ],
        out_shape=[
            jax.ShapeDtypeStruct((8, 64, 128), BF16),
            jax.ShapeDtypeStruct((64, WIDTH), BF16),
        ],
        scratch_shapes=[pltpu.VMEM((64, 128), F32), pltpu.VMEM((64, 128), F32)],
        name="kv_project",
    )(places, inv, tokens, kvw, kvw, wq)


class Ring:
    def __init__(self, at, me, right, left, send, recv, first):
        self.at, self.me, self.right, self.left = at, me, right, left
        self.send, self.recv, self.first = send, recv, first
        self.prev, self.next, self.opp = (me + 3) % 4, (me + 1) % 4, (me + 2) % 4

    def copy(self, piece, half, target, k):
        ref = self.at(piece, half)
        return pltpu.make_async_remote_copy(
            src_ref=ref,
            dst_ref=ref,
            send_sem=self.send.at[self.first + k],
            recv_sem=self.recv.at[self.first + k],
            device_id=target,
            device_id_type=MESH,
        )

    def start(self):
        self.copy(self.me, 0, self.right, 0).start()
        self.copy(self.me, 1, self.left, 2).start()
        self.copy(self.me, 1, self.right, 1).start()
        self.copy(self.me, 0, self.left, 3).start()

    def forward(self):
        self.copy(self.prev, 0, self.right, 0).wait_recv()
        self.copy(self.prev, 0, self.right, 4).start()
        self.copy(self.next, 1, self.left, 2).wait_recv()
        self.copy(self.next, 1, self.left, 5).start()

    def near(self):
        self.copy(self.prev, 1, self.right, 1).wait_recv()
        self.copy(self.next, 0, self.left, 3).wait_recv()

    def far(self):
        self.copy(self.opp, 0, self.right, 4).wait_recv()
        self.copy(self.opp, 1, self.left, 5).wait_recv()

    def drain(self):
        self.copy(self.me, 0, self.right, 0).wait_send()
        self.copy(self.me, 1, self.right, 1).wait_send()
        self.copy(self.me, 1, self.left, 2).wait_send()
        self.copy(self.me, 0, self.left, 3).wait_send()
        self.copy(self.prev, 0, self.right, 4).wait_send()
        self.copy(self.next, 1, self.left, 5).wait_send()


def gather_kernel(tok_hbm, wqt_hbm, kvp_hbm, tok, wts, kv, kvp, lsem, send, recv, zsend, zrecv, psend, precv):
    z, y, x, c = place()
    o = 1 - c
    a, b = x * o + y * c, y * o + x * c
    partner = dev(z, y, x, o)
    ring_y = (dev(z, (y + 1) % 4, x, c), dev(z, (y + 3) % 4, x, c))
    ring_x = (dev(z, y, (x + 1) % 4, c), dev(z, y, (x + 3) % 4, c))
    others = [dev((z + d) % 8, y, x, c) for d in range(1, 8)]

    own = [
        pltpu.make_async_copy(tok_hbm, tok.at[y], lsem.at[0]),
        pltpu.make_async_copy(wqt_hbm, wts.at[x, c], lsem.at[1]),
        pltpu.make_async_copy(kvp_hbm, kvp, lsem.at[2]),
        pltpu.make_async_copy(kvp_hbm.at[z], kv.at[c, b, a, z], lsem.at[3]),
    ]
    for copy in own:
        copy.start()
    barrier_with([*ring_y, *ring_x, partner, *others])

    tok_ring = Ring(lambda p, h: tok.at[p, h], y, *ring_y, send, recv, 0)
    wts_ring = Ring(lambda p, h: wts.at[p, c, h], x, *ring_x, send, recv, 6)
    near = [
        dev(z, (y + c) % 4, (x + o) % 4, c),
        dev(z, (y + 3 * c) % 4, (x + 3 * o) % 4, c),
    ]
    wide = [
        dev(z, (y + o) % 4, (x + c) % 4, c),
        dev(z, (y + 3 * o) % 4, (x + 3 * c) % 4, c),
    ]
    kv1_ring = Ring(lambda p, h: kv.at[c, b, p, pl.ds(4 * h, 4)], a, *near, send, recv, 12)
    kv2_ring = Ring(lambda p, h: kv.at[c, p, :, pl.ds(4 * h, 4)], b, *wide, send, recv, 18)

    def to_partner(ref, k):
        return pltpu.make_async_remote_copy(
            src_ref=ref,
            dst_ref=ref,
            send_sem=psend.at[k],
            recv_sem=precv.at[k],
            device_id=partner,
            device_id_type=MESH,
        )

    own[0].wait()
    tok_ring.start()
    own[1].wait()
    wts_ring.start()
    to_partner(wts.at[x, c], 0).start()
    own[2].wait()
    own[3].wait()
    zs = []
    for d in range(1, 8):
        zz = (z + d) % 8
        copy = pltpu.make_async_remote_copy(
            src_ref=kvp.at[zz],
            dst_ref=kv.at[c, b, a, z],
            send_sem=zsend.at[d - 1],
            recv_sem=zrecv.at[d - 1],
            device_id=others[d - 1],
            device_id_type=MESH,
        )
        copy.start()
        zs.append(copy)
    for d in range(1, 8):
        zz = (z + 8 - d) % 8
        pltpu.make_async_remote_copy(
            src_ref=kvp.at[zz],
            dst_ref=kv.at[c, b, a, zz],
            send_sem=zsend.at[d - 1],
            recv_sem=zrecv.at[d - 1],
            device_id=others[d - 1],
            device_id_type=MESH,
        ).wait_recv()
    kv1_ring.start()

    wts_ring.forward()
    tok_ring.forward()
    wts_ring.near()
    to_partner(wts.at[(x + 3) % 4, c], 1).start()
    to_partner(wts.at[(x + 1) % 4, c], 2).start()
    tok_ring.near()
    kv1_ring.forward()
    kv1_ring.near()
    kv1_ring.far()
    kv2_ring.start()
    to_partner(kv.at[c, b], 4).start()
    wts_ring.far()
    to_partner(wts.at[(x + 2) % 4, c], 3).start()
    tok_ring.far()
    kv2_ring.forward()
    kv2_ring.near()
    to_partner(kv.at[c, (b + 3) % 4], 5).start()
    to_partner(kv.at[c, (b + 1) % 4], 6).start()
    kv2_ring.far()
    to_partner(kv.at[c, (b + 2) % 4], 7).start()

    def from_partner(ref, k):
        pltpu.make_async_remote_copy(
            src_ref=ref,
            dst_ref=ref,
            send_sem=psend.at[k],
            recv_sem=precv.at[k],
            device_id=partner,
            device_id_type=MESH,
        ).wait_recv()

    from_partner(wts.at[x, o], 0)
    from_partner(wts.at[(x + 3) % 4, o], 1)
    from_partner(wts.at[(x + 1) % 4, o], 2)
    from_partner(wts.at[(x + 2) % 4, o], 3)
    from_partner(kv.at[o, a], 4)
    from_partner(kv.at[o, (a + 3) % 4], 5)
    from_partner(kv.at[o, (a + 1) % 4], 6)
    from_partner(kv.at[o, (a + 2) % 4], 7)
    for ring in (tok_ring, wts_ring, kv1_ring, kv2_ring):
        ring.drain()
    for copy in zs:
        copy.wait_send()
    to_partner(wts.at[x, c], 0).wait_send()
    to_partner(wts.at[(x + 3) % 4, c], 1).wait_send()
    to_partner(wts.at[(x + 1) % 4, c], 2).wait_send()
    to_partner(wts.at[(x + 2) % 4, c], 3).wait_send()
    to_partner(kv.at[c, b], 4).wait_send()
    to_partner(kv.at[c, (b + 3) % 4], 5).wait_send()
    to_partner(kv.at[c, (b + 1) % 4], 6).wait_send()
    to_partner(kv.at[c, (b + 2) % 4], 7).wait_send()


def gather(tokens, wqt, kvp):
    return pl.pallas_call(
        gather_kernel,
        in_specs=[HBM, HBM, HBM],
        out_specs=[VMEM, VMEM, VMEM],
        out_shape=[
            jax.ShapeDtypeStruct((4, 2, 32, WIDTH), BF16),
            jax.ShapeDtypeStruct((4, 2, 2, 32, WIDTH), BF16),
            jax.ShapeDtypeStruct((2, 4, 4, 8, 64, 128), BF16),
        ],
        scratch_shapes=[
            pltpu.VMEM((8, 64, 128), BF16),
            pltpu.SemaphoreType.DMA((4,)),
            pltpu.SemaphoreType.DMA((24,)),
            pltpu.SemaphoreType.DMA((24,)),
            pltpu.SemaphoreType.DMA((7,)),
            pltpu.SemaphoreType.DMA((7,)),
            pltpu.SemaphoreType.DMA((8,)),
            pltpu.SemaphoreType.DMA((8,)),
        ],
        compiler_params=pltpu.CompilerParams(collective_id=1, has_side_effects=True),
        name="gather",
    )(tokens.reshape(2, 32, WIDTH), wqt.reshape(2, 32, WIDTH), kvp)


def query_kernel(places, inv_ref, tok, wts, out, stage, send, recv):
    z, y, x, c = place()
    peers = [
        dev((z + dz) % 8, (y + dy) % 4, x, c)
        for dz in range(8)
        for dy in range(4)
        if dz or dy
    ]
    sem = pltpu.get_barrier_semaphore()
    for peer in peers:
        pl.semaphore_signal(sem, inc=1, device_id=peer, device_id_type=MESH)

    lane = lax.broadcasted_iota(I32, (32, 256), 1)
    row_block = jnp.where(
        lane < 128,
        jnp.where(lane < 64, places[z * 4], places[z * 4 + 1]),
        jnp.where(lane < 192, places[z * 4 + 2], places[z * 4 + 3]),
    )
    pos = row_block * BLK + (x * 2 + c) * 64 + lane % 64
    angle = pos.astype(F32) * jnp.concatenate([inv_ref[...], inv_ref[...]], axis=1)
    cosine, sine = jnp.cos(angle), jnp.sin(angle)
    t = tok[...].reshape(256, WIDTH)

    def target(k):
        return 2 * y + k // 4, k % 4

    def message(k):
        zz, yy = target(k)
        return pltpu.make_async_remote_copy(
            src_ref=stage.at[k],
            dst_ref=out.at[z],
            send_sem=send.at[k],
            recv_sem=recv.at[z],
            device_id=dev(zz, yy, x, c),
            device_id_type=MESH,
        )

    def away(k):
        zz, yy = target(k)
        return jnp.logical_or(zz != z, yy != y)

    for half in range(2):
        w = wts[2 * half : 2 * half + 2].reshape(256, WIDTH)
        q = dot(w, t, 1, 1)
        for i in range(4):
            k = half * 4 + i
            lo, hi = q[i * 64 : i * 64 + 32], q[i * 64 + 32 : i * 64 + 64]
            stage[k, :32] = (lo * cosine - hi * sine).astype(BF16)
            stage[k, 32:] = (hi * cosine + lo * sine).astype(BF16)
        if half == 0:
            pl.semaphore_wait(sem, len(peers))
        for i in range(4):
            k = half * 4 + i

            @pl.when(away(k))
            def _():
                message(k).start()

            @pl.when(jnp.logical_not(away(k)))
            def _():
                out[z] = stage[k]

    for g in range(8):

        @pl.when(jnp.logical_or(g != z, z // 2 != y))
        def _():
            pltpu.make_async_remote_copy(
                src_ref=stage.at[0],
                dst_ref=out.at[g],
                send_sem=send.at[0],
                recv_sem=recv.at[g],
                device_id=dev(g, z // 2, x, c),
                device_id_type=MESH,
            ).wait_recv()

    for k in range(8):

        @pl.when(away(k))
        def _():
            message(k).wait_send()


def query_project(places, tok, wts):
    inv = jnp.asarray(np.tile(INVERSE[:, None], (1, 128)))
    return pl.pallas_call(
        query_kernel,
        in_specs=[SMEM, VMEM, VMEM, VMEM],
        out_specs=VMEM,
        out_shape=jax.ShapeDtypeStruct((8, 64, 256), BF16),
        scratch_shapes=[
            pltpu.VMEM((8, 64, 256), BF16),
            pltpu.SemaphoreType.DMA((8,)),
            pltpu.SemaphoreType.DMA((8,)),
        ],
        compiler_params=pltpu.CompilerParams(collective_id=2, has_side_effects=True),
        name="query_project",
    )(places, inv, tok, wts)


def attend_kernel(places, sinks, q_ref, kv_ref, o_ref, order, vt, qt, gap, s0, s1):
    z, y, x, c = place()
    offset = (x * 2 + c) * 64
    for b in range(NBLK):
        order[places[b]] = b
    sink = sinks[z * 4 + y] * math.log2(math.e)

    key = lax.broadcasted_iota(I32, (BLK, 256), 0)
    col = lax.broadcasted_iota(I32, (BLK, 256), 1)
    key = ((key >> 6) & 3) * 128 + (key >> 8) * 64 + (key & 63)
    gap[...] = key - ((col >> 6) * BLK + offset + (col & 63))

    def keys_of(i):
        b = order[i]
        g, r = b // 4, b % 4
        k0 = kv_ref[0, r, :, g].reshape(256, 128)
        k1 = kv_ref[1, :, r, g].reshape(256, 128)
        return jnp.concatenate([k0, k1], axis=0)

    row = lax.broadcasted_iota(I32, (80, 128), 0)
    pick = jnp.logical_and(row < 64, lax.broadcasted_iota(I32, (80, 128), 1) == row + 64)
    pick = jnp.where(pick, 1.0, 0.0).astype(BF16)
    wide_row = lax.broadcasted_iota(I32, (80, BLK), 0)

    def values_of(i, _):
        vt[i] = jnp.where(wide_row < 64, dot(pick, keys_of(i), 1, 1), 1.0).astype(BF16)
        return 0

    lax.fori_loop(0, NBLK, values_of, 0)
    lane = lax.broadcasted_iota(I32, (64, 256), 1)

    def tile(j, _):
        q = jnp.zeros((64, 256), F32)
        for a in range(4):
            b = order[4 * j + a]
            part = pltpu.roll(q_ref[b // 4].astype(F32), ((a + 4 - b % 4) % 4) * 64, 1)
            q = jnp.where(lane >> 6 == a, part, q)
        qt[:64] = q.astype(BF16)
        qt[64:] = jnp.zeros((64, 256), BF16)

        def produce(i, s, masked):
            scores = dot(keys_of(i), qt[...], 1, 0) * SCALE_LOG2
            if masked:
                scores = jnp.where(gap[...] <= (4 * j - i) * BLK, scores, NEG)
            s[...] = scores
            return jnp.max(scores, axis=0, keepdims=True)

        def consume(i, s, peak, m, acc):
            new = jnp.maximum(m, peak)
            w = jnp.exp2(s[...] - new).astype(BF16)
            return new, acc * jnp.exp2(m - new) + dot(vt[i], w, 1, 0)

        def pair(masked):
            def step(t, carry):
                m, acc, peak0 = carry
                peak1 = produce(2 * t + 1, s1, masked)
                m, acc = consume(2 * t, s0, peak0, m, acc)
                peak0 = produce(2 * t + 2, s0, masked)
                m, acc = consume(2 * t + 1, s1, peak1, m, acc)
                return m, acc, peak0

            return step

        m = jnp.full((1, 256), sink, F32)
        acc = jnp.where(lax.broadcasted_iota(I32, (80, 256), 0) < 64, 0.0, 1.0)
        peak = produce(0, s0, True)
        free = jnp.maximum(2 * j - 1, 0)
        carry = lax.fori_loop(0, free, pair(False), (m, acc, peak))
        m, acc, peak0 = lax.fori_loop(free, 2 * j + 1, pair(True), carry)
        peak1 = produce(4 * j + 3, s1, True)
        m, acc = consume(4 * j + 2, s0, peak0, m, acc)
        m, acc = consume(4 * j + 3, s1, peak1, m, acc)

        out = acc[:64] / acc[64:65]
        out = jnp.concatenate([out, jnp.zeros((64, 256), F32)], axis=0).T
        for a in range(4):
            top, low = out[64 * a : 64 * a + 32], out[64 * a + 32 : 64 * a + 64]
            o_ref[order[4 * j + a]] = (top + pltpu.roll(low, 64, 1)).astype(BF16)
        return 0

    lax.fori_loop(0, NBLK // 4, tile, 0)


def attend(places, sinks, q, kv):
    return pl.pallas_call(
        attend_kernel,
        in_specs=[SMEM, SMEM, VMEM, VMEM],
        out_specs=VMEM,
        out_shape=jax.ShapeDtypeStruct((NBLK, 32, 128), BF16),
        scratch_shapes=[
            pltpu.SMEM((NBLK,), I32),
            pltpu.VMEM((NBLK, 80, BLK), BF16),
            pltpu.VMEM((128, 256), BF16),
            pltpu.VMEM((BLK, 256), I32),
            pltpu.VMEM((BLK, 256), F32),
            pltpu.VMEM((BLK, 256), F32),
        ],
        name="attend",
    )(places, sinks, q, kv)


def return_kernel(o_hbm, out, held, own, lsem, send, recv):
    z, y, x, c = place()
    offsets = [(dz, dy) for dz in range(8) for dy in range(4) if dz or dy]
    local = [
        pltpu.make_async_copy(o_hbm, own, lsem.at[0]),
        pltpu.make_async_copy(o_hbm.at[z * 4 + y], held.at[z * 4 + y], lsem.at[1]),
    ]
    for copy in local:
        copy.start()
    barrier_with([dev((z + dz) % 8, (y + dy) % 4, x, c) for dz, dy in offsets])
    for copy in local:
        copy.wait()
    copies = []
    for k, (dz, dy) in enumerate(offsets):
        zz, yy = (z + dz) % 8, (y + dy) % 4
        copy = pltpu.make_async_remote_copy(
            src_ref=own.at[zz * 4 + yy],
            dst_ref=held.at[z * 4 + y],
            send_sem=send.at[k],
            recv_sem=recv.at[k],
            device_id=dev(zz, yy, x, c),
            device_id_type=MESH,
        )
        copy.start()
        copies.append(copy)
    for k, (dz, dy) in enumerate(offsets):
        zz, yy = (z + 8 - dz) % 8, (y + 4 - dy) % 4
        pltpu.make_async_remote_copy(
            src_ref=own.at[0],
            dst_ref=held.at[zz * 4 + yy],
            send_sem=send.at[k],
            recv_sem=recv.at[k],
            device_id=dev(zz, yy, x, c),
            device_id_type=MESH,
        ).wait_recv()
    lane = lax.broadcasted_iota(I32, (32, 128), 1)
    for k in range(16):
        p, q = held[2 * k].astype(F32), held[2 * k + 1].astype(F32)
        cols = pl.ds(128 * k, 128)
        out[:32, cols] = jnp.where(lane < 64, p, pltpu.roll(q, 64, 1)).astype(BF16)
        out[32:, cols] = jnp.where(lane < 64, pltpu.roll(p, 64, 1), q).astype(BF16)
    for copy in copies:
        copy.wait_send()


def send_back(o):
    return pl.pallas_call(
        return_kernel,
        in_specs=[HBM],
        out_specs=VMEM,
        out_shape=jax.ShapeDtypeStruct((64, 2048), BF16),
        scratch_shapes=[
            pltpu.VMEM((NBLK, 32, 128), BF16),
            pltpu.VMEM((NBLK, 32, 128), BF16),
            pltpu.SemaphoreType.DMA((2,)),
            pltpu.SemaphoreType.DMA((31,)),
            pltpu.SemaphoreType.DMA((31,)),
        ],
        compiler_params=pltpu.CompilerParams(collective_id=3, has_side_effects=True),
        name="send_back",
    )(o)


def per_device(tokens, query_weight, key_value_weight, block_places, sinks):
    kvp, wqt = kv_project(block_places, tokens, key_value_weight, query_weight)
    tok, wts, kv = gather(tokens, wqt, kvp)
    q = query_project(block_places, tok, wts)
    o = attend(block_places, sinks, q, kv)
    return send_back(o)


def solution(mesh):
    in_specs = (P(("grp", "sp"), None), P(None, "sp"), P(), P(), P())
    return jax.shard_map(
        per_device,
        mesh=mesh,
        in_specs=in_specs,
        out_specs=P(("grp", "sp"), None),
        check_vma=False,
    )
```

time: 354 us -> 144 us (0.41)
  waiting for transfers between devices: 160 us -> 0 us
  Pallas kernels: 0 us -> 140 us
  matrix products: 103 us -> 0 us
  other arithmetic: 47.6 us -> 0 us
  blocking collectives: 16.4 us -> 0 us
  between operations: 13.3 us -> 0.03 us
  local copies, waits for them, and re-layouts: 12.9 us -> 3.8 us
    all_gather x3 -> x0, waiting for transfers between devices: 159 us -> none  [the longest x2 106 us: piecewise(): finished.append(jax.vmap(apply)(lax.all_gather(share, axis), starts))]
    pallas_call x0 -> x5, Pallas kernels: none -> 140 us  [the longest x1 49.3 us: attend(): pl.pallas_call(attend_kernel, in_specs=[SMEM, SMEM, VMEM, VMEM], out_spec...]
    dot_general x18 -> x0, matrix products: 103 us -> none  [the longest x8 65 us: attend(): jnp.einsum('hgqk,khd->hgqd', weights.astype(jnp.bfloat16), value_part, pr...]
    reduce_sum x17 -> x0, other arithmetic: 43.5 us -> none  [the longest x8 42.5 us: attend(): totals = totals * factor + jnp.sum(weights, axis=-1)]
    all_to_all x1 -> x0, blocking collectives: 16.4 us -> none  [per_device(): lax.all_to_all(attended, 'sp', split_axis=0, concat_axis=1, tiled=True)]
    while x26 -> x0, local copies, waits for them, and re-layouts: 3.98 us -> none
  transfers between devices with their start and end apart: 3 -> 0, of which waited for: 3 -> 0; matrix products, arithmetic and copies ran while one was open for 2% -> 0% of each run, Pallas kernels for 0% -> 0%
where the time goes in v1:
time: 144 us
  Pallas kernels  140 us (97%)
  local copies, waits for them, and re-layouts  3.8 us (3%)
    pallas_call x1, Pallas kernels, attend(): pl.pallas_call(attend_kernel, in_specs=[SMEM, SMEM, VMEM, VMEM], out_spec...  49.3 us
    pallas_call x1, Pallas kernels, gather(): pl.pallas_call(gather_kernel, in_specs=[HBM, HBM, HBM], out_specs=[VMEM,...  44.6 us
    pallas_call x1, Pallas kernels, send_back(): pl.pallas_call(return_kernel, in_specs=[HBM], out_specs=VMEM, out_shape=j...  29 us
    pallas_call x1, Pallas kernels, query_project(): pl.pallas_call(query_kernel, in_specs=[SMEM, VMEM, VMEM, VMEM], out_specs...  11.7 us
    pallas_call x1, Pallas kernels, kv_project(): pl.pallas_call(kv_kernel, grid=(4,), in_specs=[SMEM, pl.BlockSpec((1, 128...  5.78 us
    unnamed x2, local copies, waits for them, and re-layouts  3.8 us

profile of v1, /device:TPU:1, one launch (start us, length us, event | category | flops | bytes accessed | tf_op | source)
XLA Modules:
  0.0 144.2 jit_solution(12308369991671548878)
XLA Ops:
  0.0 2.1 %copy.8.wq_ref = bf16[2880,64]{1,0:T(8,128)(2,1)} copy(bf16[2880,64]{0,1:T(8,128)(2,1)} %param.8) | data formatting | bytes 737280 | tf_op args[1]
  2.1 5.8 %kv_project.1 = (bf16[8,64,128]{2,1,0:T(8,128)(2,1)}, bf16[64,2880]{1,0:T(8,128)(2,1)}) custom-call(s32[32]{0:T(128)} %places.5, f32[1,128]{1,0:T(1,128)} %constant.4.clone.inv_ref, bf16[64,2880]{1,0:T(8,128)(2,1)} %tok_ref.1, bf16[2880,1024]{1,0:T(8,128)(2,1)} %wv_ref.1, bf16[2880,1024]{1,0:T(8,128)(2,1)} %wv_ref.1, bf16[2880,64]{1,0:T(8,128)(2,1)} %copy.8.wq_ref), custom_call_target="tpu_custom_call" | custom-call | tf_op jit(solution)/shard_map/kv_project/pallas_call | solution.py:72
  7.9 44.6 %gather.1 = (bf16[4,2,32,2880]{3,2,1,0:T(8,128)(2,1)}, bf16[4,2,2,32,2880]{4,3,2,1,0:T(8,128)(2,1)}, bf16[2,4,4,8,64,128]{5,4,3,2,1,0:T(8,128)(2,1)}) custom-call(bf16[2,32,2880]{2,1,0:T(8,128)(2,1)} %bitcast.2, bf16[2,32,2880]{2,1,0:T(8,128)(2,1)} %bitcast.3, bf16[8,64,128]{2,1,0:T(8,128)(2,1)} %get-tuple-element.11.kvp_hbm), custom_call_target="tpu_custom_call" | custom-call | tf_op jit(solution)/shard_map/gather/pallas_call | solution.py:270
  52.5 11.7 %query_project.1.q_ref = bf16[8,64,256]{2,1,0:T(8,128)(2,1)} custom-call(s32[32]{0:T(128)} %places.5, f32[32,128]{1,0:T(8,128)} %constant.5.clone.inv_ref, bf16[4,2,32,2880]{3,2,1,0:T(8,128)(2,1)} %get-tuple-element.12.tok, bf16[4,2,2,32,2880]{4,3,2,1,0:T(8,128)(2,1)} %get-tuple-element.13.wts), custom_call_target="tpu_custom_call" | custom-call | tf_op jit(solution)/shard_map/query_project/pallas_call | solution.py:378
  64.2 49.3 %attend.1.o_hbm = bf16[32,32,128]{2,1,0:T(8,128)(2,1)} custom-call(s32[32]{0:T(128)} %places.5, f32[32]{0:T(128)} %sinks.1, bf16[8,64,256]{2,1,0:T(8,128)(2,1)} %query_project.1.q_ref, bf16[2,4,4,8,64,128]{5,4,3,2,1,0:T(8,128)(2,1)} %get-tuple-element.14.kv_ref), custom_call_target="tpu_custom_call" | custom-call | tf_op jit(solution)/shard_map/attend/pallas_call | solution.py:477
  113.5 29.0 %send_back.1 = bf16[64,2048]{1,0:T(8,128)(2,1)} custom-call(bf16[32,32,128]{2,1,0:T(8,128)(2,1)} %attend.1.o_hbm), custom_call_target="tpu_custom_call" | custom-call | tf_op jit(solution)/shard_map/send_back/pallas_call | solution.py:540
  142.5 1.7 %copy.10 = bf16[64,2048]{1,0:T(8,128)(2,1)} copy(bf16[64,2048]{1,0:T(8,128)(2,1)} %send_back.1) | data formatting | bytes 524288

commit v2 on v1

v2 whole, which is shorter than its diff:
```python
import math

import jax
import jax.numpy as jnp
import numpy as np
from jax import lax
from jax.experimental import pallas as pl
from jax.experimental.pallas import tpu as pltpu
from jax.sharding import PartitionSpec as P

MESH = pl.DeviceIdType.MESH
BF16, F32, I32 = jnp.bfloat16, jnp.float32, jnp.int32
WIDTH = 2880
HEAD = 64
BLK = 512
NBLK = 32
SCALE_LOG2 = HEAD**-0.5 * math.log2(math.e)
NEG = -1e30
VMEM = pl.BlockSpec(memory_space=pltpu.VMEM)
HBM = pl.BlockSpec(memory_space=pltpu.HBM)
SMEM = pl.BlockSpec(memory_space=pltpu.SMEM)
OFFSETS = [(dz, dy) for dz in range(8) for dy in range(4) if dz or dy]
INVERSE = (150000.0 ** (-(np.arange(32, dtype=np.float64) * 2.0) / HEAD)).astype(np.float32)


def place():
    z = lax.axis_index("grp")
    s = lax.axis_index("sp")
    return z, s // 8, (s // 2) % 4, s % 2


def dev(z, y, x, c):
    return (z, (y * 4 + x) * 2 + c)


def dot(a, b, ca, cb):
    return lax.dot_general(a, b, (((ca,), (cb,)), ((), ())), preferred_element_type=F32)


def barrier_with(peers):
    sem = pltpu.get_barrier_semaphore()
    for peer in peers:
        pl.semaphore_signal(sem, inc=1, device_id=peer, device_id_type=MESH)
    pl.semaphore_wait(sem, len(peers))


class Ring:
    def __init__(self, at, me, right, left, send, recv, first):
        self.at, self.me, self.right, self.left = at, me, right, left
        self.send, self.recv, self.first = send, recv, first
        self.prev, self.next, self.opp = (me + 3) % 4, (me + 1) % 4, (me + 2) % 4

    def copy(self, piece, half, target, k):
        ref = self.at(piece, half)
        return pltpu.make_async_remote_copy(
            src_ref=ref,
            dst_ref=ref,
            send_sem=self.send.at[self.first + k],
            recv_sem=self.recv.at[self.first + k],
            device_id=target,
            device_id_type=MESH,
        )

    def start(self):
        self.copy(self.me, 0, self.right, 0).start()
        self.copy(self.me, 1, self.left, 2).start()
        self.copy(self.me, 1, self.right, 1).start()
        self.copy(self.me, 0, self.left, 3).start()

    def forward(self):
        self.copy(self.prev, 0, self.right, 0).wait_recv()
        self.copy(self.prev, 0, self.right, 4).start()
        self.copy(self.next, 1, self.left, 2).wait_recv()
        self.copy(self.next, 1, self.left, 5).start()

    def near(self):
        self.copy(self.prev, 1, self.right, 1).wait_recv()
        self.copy(self.next, 0, self.left, 3).wait_recv()

    def far(self):
        self.copy(self.opp, 0, self.right, 4).wait_recv()
        self.copy(self.opp, 1, self.left, 5).wait_recv()

    def drain(self):
        self.copy(self.me, 0, self.right, 0).wait_send()
        self.copy(self.me, 1, self.right, 1).wait_send()
        self.copy(self.me, 1, self.left, 2).wait_send()
        self.copy(self.me, 0, self.left, 3).wait_send()
        self.copy(self.prev, 0, self.right, 4).wait_send()
        self.copy(self.next, 1, self.left, 5).wait_send()


def prepare_kernel(
    places, inv_row, inv_col, tok_hbm, wqt_hbm, kvw_hbm, q_out, kv,
    tok, wts, kvw, kvp, stage, angles, lsem, send, recv, zsend, zrecv, psend, precv, qsend, qrecv,
):
    z, y, x, c = place()
    o = 1 - c
    a, b = x * o + y * c, y * o + x * c
    partner = dev(z, y, x, o)
    ring_y = (dev(z, (y + 1) % 4, x, c), dev(z, (y + 3) % 4, x, c))
    ring_x = (dev(z, y, (x + 1) % 4, c), dev(z, y, (x + 3) % 4, c))
    others = [dev((z + d) % 8, y, x, c) for d in range(1, 8)]
    peers = [dev((z + dz) % 8, (y + dy) % 4, x, c) for dz, dy in OFFSETS]
    peers += [*ring_x, partner]

    ready = pltpu.get_barrier_semaphore()
    for peer in peers:
        pl.semaphore_signal(ready, inc=1, device_id=peer, device_id_type=MESH)

    own = [
        pltpu.make_async_copy(tok_hbm, tok.at[y], lsem.at[0]),
        pltpu.make_async_copy(wqt_hbm, wts.at[x, c], lsem.at[1]),
    ]
    for n in range(4):
        cols = pl.ds(256 * n, 256)
        own.append(pltpu.make_async_copy(kvw_hbm.at[:, cols], kvw.at[:, cols], lsem.at[2 + n]))
    for n in (0, 1, 2, 4, 3, 5):
        own[n].start()

    lane = lax.broadcasted_iota(I32, (64, 128), 1)
    base = places[z * 4 + y] * BLK + (x * 2 + c) * 64
    angle = (base + lax.broadcasted_iota(I32, (64, 128), 0)).astype(F32) * inv_row[...]
    cosine = jnp.cos(angle)
    sine = jnp.where(lane % 64 < 32, -1.0, 1.0) * jnp.sin(angle)
    own[0].wait()
    rows = tok[y].reshape(64, WIDTH)
    for n in range(2):
        own[2 + n].wait()
        own[4 + n].wait()
        keys = jnp.dot(rows, kvw[:, 256 * n : 256 * n + 256], preferred_element_type=F32)
        values = jnp.dot(rows, kvw[:, 512 + 256 * n : 768 + 256 * n], preferred_element_type=F32)
        for p in range(2):
            k, v = keys[:, 128 * p : 128 * p + 128], values[:, 128 * p : 128 * p + 128]
            swapped = jnp.where(lane % 64 < 32, pltpu.roll(k, 96, 1), pltpu.roll(k, 32, 1))
            k = k * cosine + swapped * sine
            kvp[4 * n + 2 * p] = jnp.where(lane < 64, k, pltpu.roll(v, 64, 1)).astype(BF16)
            kvp[4 * n + 2 * p + 1] = jnp.where(lane < 64, pltpu.roll(k, 64, 1), v).astype(BF16)
    kv[c, b, a, z] = kvp[z]

    col = lax.broadcasted_iota(I32, (32, 256), 1)
    block = jnp.where(
        col < 128,
        jnp.where(col < 64, places[z * 4], places[z * 4 + 1]),
        jnp.where(col < 192, places[z * 4 + 2], places[z * 4 + 3]),
    )
    angle = (block * BLK + (x * 2 + c) * 64 + col % 64).astype(F32)
    angle = angle * jnp.concatenate([inv_col[...], inv_col[...]], axis=1)
    angles[0], angles[1] = jnp.cos(angle), jnp.sin(angle)
    own[1].wait()
    pl.semaphore_wait(ready, len(peers))

    tok_ring = Ring(lambda p, h: tok.at[p, h], y, *ring_y, send, recv, 0)
    wts_ring = Ring(lambda p, h: wts.at[p, c, h], x, *ring_x, send, recv, 6)
    near = [
        dev(z, (y + c) % 4, (x + o) % 4, c),
        dev(z, (y + 3 * c) % 4, (x + 3 * o) % 4, c),
    ]
    wide = [
        dev(z, (y + o) % 4, (x + c) % 4, c),
        dev(z, (y + 3 * o) % 4, (x + 3 * c) % 4, c),
    ]
    kv1_ring = Ring(lambda p, h: kv.at[c, b, p, pl.ds(4 * h, 4)], a, *near, send, recv, 12)
    kv2_ring = Ring(lambda p, h: kv.at[c, p, :, pl.ds(4 * h, 4)], b, *wide, send, recv, 18)

    def with_partner(ref, k):
        return pltpu.make_async_remote_copy(
            src_ref=ref,
            dst_ref=ref,
            send_sem=psend.at[k],
            recv_sem=precv.at[k],
            device_id=partner,
            device_id_type=MESH,
        )

    def exchange(d, head, source):
        return pltpu.make_async_remote_copy(
            src_ref=kvp.at[head],
            dst_ref=kv.at[c, b, a, source],
            send_sem=zsend.at[d - 1],
            recv_sem=zrecv.at[d - 1],
            device_id=others[d - 1],
            device_id_type=MESH,
        )

    tok_ring.start()
    wts_ring.start()
    for d in range(1, 8):
        exchange(d, (z + d) % 8, z).start()
    with_partner(wts.at[x, c], 0).start()
    for d in range(1, 8):
        exchange(d, z, (z + 8 - d) % 8).wait_recv()
    kv1_ring.start()

    wts_ring.forward()
    tok_ring.forward()
    wts_ring.near()
    with_partner(wts.at[(x + 3) % 4, c], 1).start()
    with_partner(wts.at[(x + 1) % 4, c], 2).start()
    tok_ring.near()
    kv1_ring.forward()
    wts_ring.far()
    with_partner(wts.at[(x + 2) % 4, c], 3).start()
    kv1_ring.near()
    kv1_ring.far()
    kv2_ring.start()
    with_partner(kv.at[c, b], 4).start()
    tok_ring.far()
    with_partner(wts.at[x, o], 0).wait_recv()
    with_partner(wts.at[(x + 3) % 4, o], 1).wait_recv()
    with_partner(wts.at[(x + 1) % 4, o], 2).wait_recv()
    with_partner(wts.at[(x + 2) % 4, o], 3).wait_recv()

    def message(k):
        return pltpu.make_async_remote_copy(
            src_ref=stage.at[k],
            dst_ref=q_out.at[z],
            send_sem=qsend.at[k],
            recv_sem=qrecv.at[z],
            device_id=dev(2 * y + k // 4, k % 4, x, c),
            device_id_type=MESH,
        )

    def away(k):
        return jnp.logical_or(2 * y + k // 4 != z, k % 4 != y)

    rows = tok[...].reshape(256, WIDTH)
    for half in range(2):
        w = wts[2 * half : 2 * half + 2].reshape(256, WIDTH)
        q = dot(w, rows, 1, 1)
        for i in range(4):
            k = half * 4 + i
            lo, hi = q[i * 64 : i * 64 + 32], q[i * 64 + 32 : i * 64 + 64]
            stage[k, :32] = (lo * angles[0] - hi * angles[1]).astype(BF16)
            stage[k, 32:] = (hi * angles[0] + lo * angles[1]).astype(BF16)
    for k in range(8):

        @pl.when(away(k))
        def _():
            message(k).start()

        @pl.when(jnp.logical_not(away(k)))
        def _():
            q_out[z] = stage[k]

    kv2_ring.forward()
    kv2_ring.near()
    with_partner(kv.at[c, (b + 3) % 4], 5).start()
    with_partner(kv.at[c, (b + 1) % 4], 6).start()
    kv2_ring.far()
    with_partner(kv.at[c, (b + 2) % 4], 7).start()

    for g in range(8):

        @pl.when(jnp.logical_or(g != z, z // 2 != y))
        def _():
            pltpu.make_async_remote_copy(
                src_ref=stage.at[0],
                dst_ref=q_out.at[g],
                send_sem=qsend.at[0],
                recv_sem=qrecv.at[g],
                device_id=dev(g, z // 2, x, c),
                device_id_type=MESH,
            ).wait_recv()

    with_partner(kv.at[o, a], 4).wait_recv()
    with_partner(kv.at[o, (a + 3) % 4], 5).wait_recv()
    with_partner(kv.at[o, (a + 1) % 4], 6).wait_recv()
    with_partner(kv.at[o, (a + 2) % 4], 7).wait_recv()
    for ring in (tok_ring, wts_ring, kv1_ring, kv2_ring):
        ring.drain()
    for d in range(1, 8):
        exchange(d, (z + d) % 8, z).wait_send()
    with_partner(wts.at[x, c], 0).wait_send()
    with_partner(wts.at[(x + 3) % 4, c], 1).wait_send()
    with_partner(wts.at[(x + 1) % 4, c], 2).wait_send()
    with_partner(wts.at[(x + 2) % 4, c], 3).wait_send()
    with_partner(kv.at[c, b], 4).wait_send()
    with_partner(kv.at[c, (b + 3) % 4], 5).wait_send()
    with_partner(kv.at[c, (b + 1) % 4], 6).wait_send()
    with_partner(kv.at[c, (b + 2) % 4], 7).wait_send()
    for k in range(8):

        @pl.when(away(k))
        def _():
            message(k).wait_send()


def prepare(places, tokens, wq, kvw):
    dma = pltpu.SemaphoreType.DMA
    return pl.pallas_call(
        prepare_kernel,
        in_specs=[SMEM, VMEM, VMEM, HBM, HBM, HBM],
        out_specs=[VMEM, VMEM],
        out_shape=[
            jax.ShapeDtypeStruct((8, 64, 256), BF16),
            jax.ShapeDtypeStruct((2, 4, 4, 8, 64, 128), BF16),
        ],
        scratch_shapes=[
            pltpu.VMEM((4, 2, 32, WIDTH), BF16),
            pltpu.VMEM((4, 2, 2, 32, WIDTH), BF16),
            pltpu.VMEM((WIDTH, 1024), BF16),
            pltpu.VMEM((8, 64, 128), BF16),
            pltpu.VMEM((8, 64, 256), BF16),
            pltpu.VMEM((2, 32, 256), F32),
            dma((6,)),
            dma((24,)),
            dma((24,)),
            dma((7,)),
            dma((7,)),
            dma((8,)),
            dma((8,)),
            dma((8,)),
            dma((8,)),
        ],
        compiler_params=pltpu.CompilerParams(collective_id=1, has_side_effects=True),
        name="prepare",
    )(
        places,
        jnp.asarray(np.tile(INVERSE, 4)[None, :]),
        jnp.asarray(np.tile(INVERSE[:, None], (1, 128))),
        tokens.reshape(2, 32, WIDTH),
        wq.T.reshape(2, 32, WIDTH),
        kvw,
    )


def attend_kernel(places, sinks, q_ref, kv_ref, o_ref, order, vt, qt, gap, s):
    z, y, x, c = place()
    offset = (x * 2 + c) * 64
    for b in range(NBLK):
        order[places[b]] = b
    sink = sinks[z * 4 + y] * math.log2(math.e)

    key = lax.broadcasted_iota(I32, (BLK, 256), 0)
    col = lax.broadcasted_iota(I32, (BLK, 256), 1)
    key = ((key >> 6) & 3) * 128 + (key >> 8) * 64 + (key & 63)
    gap[...] = key - ((col >> 6) * BLK + offset + (col & 63))

    def keys_of(i):
        b = order[i]
        g, r = b // 4, b % 4
        return kv_ref[0, r, :, g].reshape(256, 128), kv_ref[1, :, r, g].reshape(256, 128)

    lane = lax.broadcasted_iota(I32, (64, 256), 1)
    zero = jnp.where(lax.broadcasted_iota(I32, (80, 256), 0) < 64, 0.0, 1.0)
    vt[...] = jnp.ones((NBLK, 2, 80, 256), BF16)

    def load_queries(first, slot):
        q = jnp.zeros((64, 256), F32)
        for a in range(4):
            b = order[first + a]
            part = pltpu.roll(q_ref[b // 4].astype(F32), ((a + 4 - b % 4) % 4) * 64, 1)
            q = jnp.where(lane >> 6 == a, part, q)
        qt[slot, :64] = q.astype(BF16)
        qt[slot, 64:] = jnp.zeros((64, 256), BF16)

    def raw_scores(i, slot):
        return [dot(keys, qt[slot], 1, 0) for keys in keys_of(i)]

    def keep(raw, limit, store):
        peaks = []
        for part, scores in enumerate(raw):
            rows = pl.ds(256 * part, 256)
            scores = scores * SCALE_LOG2
            if limit is not None:
                scores = jnp.where(gap[rows] <= limit, scores, NEG)
            store[rows] = scores
            peaks.append(jnp.max(scores, axis=0, keepdims=True))
        return jnp.maximum(*peaks)

    def weigh(i, store, m, acc):
        for part in range(2):
            w = jnp.exp2(store[256 * part : 256 * part + 256] - m).astype(BF16)
            acc = acc + dot(vt[i, part], w, 1, 0)
        return acc

    def step(i, states):
        raw = [raw_scores(i + 1, slot) for slot in range(2)]
        done = []
        for slot in range(2):
            m, acc, peak = states[slot]
            new = jnp.maximum(m, peak)
            acc = weigh(i, s.at[slot], new, acc * jnp.exp2(m - new))
            done.append((new, acc, keep(raw[slot], None, s.at[slot])))
        return tuple(done)

    def finish(first, acc):
        out = acc[:64] / acc[64:65]
        out = jnp.concatenate([out, jnp.zeros((64, 256), F32)], axis=0).T
        for a in range(4):
            top, low = out[64 * a : 64 * a + 32], out[64 * a + 32 : 64 * a + 64]
            o_ref[order[first + a]] = (top + pltpu.roll(low, 64, 1)).astype(BF16)

    def tiles(j, _):
        base = 8 * j
        for slot in range(2):
            load_queries(base + 4 * slot, slot)
        def turn(i):
            for part, keys in enumerate(keys_of(i)):
                vt[i, part, :64] = keys.T[64:]

        def three(u):
            first = jnp.where(u == 4, 0, base + u)
            last = jnp.where(u == 4, 0, base + 4 + u)
            limit = jnp.where(u == 4, 32 * BLK, -u * BLK)
            raw = raw_scores(first, 0), raw_scores(first, 1), raw_scores(last, 1)
            return raw, (limit, None, limit)

        def keep_three(raw, limits):
            return tuple(keep(raw[n], limits[n], s.at[n]) for n in range(3))

        def near(u, carry):
            (m0, acc0), (m1, acc1), (p0, p1, p2) = carry
            raw, limits = three(u + 1)
            turn(base + u)
            turn(base + 4 + u)
            n0 = jnp.maximum(m0, p0)
            n1 = jnp.maximum(m1, jnp.maximum(p1, p2))
            acc0 = weigh(base + u, s.at[0], n0, acc0 * jnp.exp2(m0 - n0))
            acc1 = weigh(base + u, s.at[1], n1, acc1 * jnp.exp2(m1 - n1))
            acc1 = weigh(base + 4 + u, s.at[2], n1, acc1)
            return (n0, acc0), (n1, acc1), keep_three(raw, limits)

        m = jnp.full((1, 256), sink, F32)
        carry = (m, zero), (m, zero), keep_three(*three(0))
        carry = lax.fori_loop(0, 2, lambda t, v: near(2 * t + 1, near(2 * t, v)), carry)
        states = tuple((*carry[slot], carry[2][slot]) for slot in range(2))

        def pair(t, states):
            return step(2 * t + 1, step(2 * t, states))

        states = lax.fori_loop(0, 4 * j, pair, states)
        for slot in range(2):
            finish(base + 4 * slot, states[slot][1])
        return 0

    lax.fori_loop(0, NBLK // 8, tiles, 0)


def attend(places, sinks, q, kv):
    return pl.pallas_call(
        attend_kernel,
        in_specs=[SMEM, SMEM, VMEM, VMEM],
        out_specs=VMEM,
        out_shape=jax.ShapeDtypeStruct((NBLK, 32, 128), BF16),
        scratch_shapes=[
            pltpu.SMEM((NBLK,), I32),
            pltpu.VMEM((NBLK, 2, 80, 256), BF16),
            pltpu.VMEM((2, 128, 256), BF16),
            pltpu.VMEM((BLK, 256), I32),
            pltpu.VMEM((3, BLK, 256), F32),
        ],
        name="attend",
    )(places, sinks, q, kv)


def return_kernel(o_hbm, out, held, own, lsem, send, recv):
    z, y, x, c = place()
    local = [
        pltpu.make_async_copy(o_hbm, own, lsem.at[0]),
        pltpu.make_async_copy(o_hbm.at[z * 4 + y], held.at[z * 4 + y], lsem.at[1]),
    ]
    for copy in local:
        copy.start()
    barrier_with([dev((z + dz) % 8, (y + dy) % 4, x, c) for dz, dy in OFFSETS])
    for copy in local:
        copy.wait()
    copies = []
    for k, (dz, dy) in enumerate(OFFSETS):
        zz, yy = (z + dz) % 8, (y + dy) % 4
        copy = pltpu.make_async_remote_copy(
            src_ref=own.at[zz * 4 + yy],
            dst_ref=held.at[z * 4 + y],
            send_sem=send.at[k],
            recv_sem=recv.at[k],
            device_id=dev(zz, yy, x, c),
            device_id_type=MESH,
        )
        copy.start()
        copies.append(copy)
    for k, (dz, dy) in enumerate(OFFSETS):
        zz, yy = (z + 8 - dz) % 8, (y + 4 - dy) % 4
        pltpu.make_async_remote_copy(
            src_ref=own.at[0],
            dst_ref=held.at[zz * 4 + yy],
            send_sem=send.at[k],
            recv_sem=recv.at[k],
            device_id=dev(zz, yy, x, c),
            device_id_type=MESH,
        ).wait_recv()
    lane = lax.broadcasted_iota(I32, (32, 128), 1)
    for k in range(16):
        p, q = held[2 * k].astype(F32), held[2 * k + 1].astype(F32)
        cols = pl.ds(128 * k, 128)
        out[:32, cols] = jnp.where(lane < 64, p, pltpu.roll(q, 64, 1)).astype(BF16)
        out[32:, cols] = jnp.where(lane < 64, pltpu.roll(p, 64, 1), q).astype(BF16)
    for copy in copies:
        copy.wait_send()


def send_back(o):
    return pl.pallas_call(
        return_kernel,
        in_specs=[HBM],
        out_specs=VMEM,
        out_shape=jax.ShapeDtypeStruct((64, 2048), BF16),
        scratch_shapes=[
            pltpu.VMEM((NBLK, 32, 128), BF16),
            pltpu.VMEM((NBLK, 32, 128), BF16),
            pltpu.SemaphoreType.DMA((2,)),
            pltpu.SemaphoreType.DMA((31,)),
            pltpu.SemaphoreType.DMA((31,)),
        ],
        compiler_params=pltpu.CompilerParams(collective_id=3, has_side_effects=True),
        name="send_back",
    )(o)


def per_device(tokens, query_weight, key_value_weight, block_places, sinks):
    q, kv = prepare(block_places, tokens, query_weight, key_value_weight)
    o = attend(block_places, sinks, q, kv)
    return send_back(o)


def solution(mesh):
    in_specs = (P(("grp", "sp"), None), P(None, "sp"), P(), P(), P())
    return jax.shard_map(
        per_device,
        mesh=mesh,
        in_specs=in_specs,
        out_specs=P(("grp", "sp"), None),
        check_vma=False,
    )
```

time: 144 us -> 100 us (0.69)
  Pallas kernels: 140 us -> 98.6 us
  local copies, waits for them, and re-layouts: 3.8 us -> 1.67 us
    pallas_call x1, Pallas kernels: 49.3 us -> 28.5 us  [attend(): pl.pallas_call(attend_kernel, in_specs=[SMEM, SMEM, VMEM, VMEM], out_spec...]
    pallas_call x1, Pallas kernels: 29 us -> 17.6 us  [send_back(): pl.pallas_call(return_kernel, in_specs=[HBM], out_specs=VMEM, out_shape=j...]
    pallas_call x3 -> x1, Pallas kernels: 62 us -> 52.5 us  [prepare(): pl.pallas_call(prepare_kernel, in_specs=[SMEM, VMEM, VMEM, HBM, HBM, HBM]...]
    unnamed x2 -> x1, local copies, waits for them, and re-layouts: 3.8 us -> 1.67 us
where the time goes in v2:
time: 100 us
  Pallas kernels  98.6 us (99%)
  local copies, waits for them, and re-layouts  1.67 us (2%)
    pallas_call x1, Pallas kernels, prepare(): pl.pallas_call(prepare_kernel, in_specs=[SMEM, VMEM, VMEM, HBM, HBM, HBM]...  52.5 us
    pallas_call x1, Pallas kernels, attend(): pl.pallas_call(attend_kernel, in_specs=[SMEM, SMEM, VMEM, VMEM], out_spec...  28.5 us
    pallas_call x1, Pallas kernels, send_back(): pl.pallas_call(return_kernel, in_specs=[HBM], out_specs=VMEM, out_shape=j...  17.6 us

profile of v2, /device:TPU:1, one launch (start us, length us, event | category | flops | bytes accessed | tf_op | source)
XLA Modules:
  0.0 100.3 jit_solution(18045905844586210114)
XLA Ops:
  0.0 52.5 %prepare.1 = (bf16[8,64,256]{2,1,0:T(8,128)(2,1)}, bf16[2,4,4,8,64,128]{5,4,3,2,1,0:T(8,128)(2,1)}) custom-call(s32[32]{0:T(128)} %places.3, f32[1,128]{1,0:T(1,128)} %constant.4.clone.inv_row, f32[32,128]{1,0:T(8,128)} %constant.5.clone.inv_col, bf16[2,32,2880]{2,1,0:T(8,128)(2,1)} %bitcast.4, bf16[2,32,2880]{2,1,0:T(8,128)(2,1)} %bitcast.5, ...), custom_call_target="tpu_custom_call" | custom-call | tf_op jit(solution)/shard_map/prepare/pallas_call | solution.py:291
  52.5 28.5 %attend.1.o_hbm = bf16[32,32,128]{2,1,0:T(8,128)(2,1)} custom-call(s32[32]{0:T(128)} %places.3, f32[32]{0:T(128)} %sinks.1, bf16[8,64,256]{2,1,0:T(8,128)(2,1)} %get-tuple-element.7.q_ref, bf16[2,4,4,8,64,128]{5,4,3,2,1,0:T(8,128)(2,1)} %get-tuple-element.8.kv_ref), custom_call_target="tpu_custom_call" | custom-call | tf_op jit(solution)/shard_map/attend/pallas_call | solution.py:442
  81.0 17.6 %send_back.1 = bf16[64,2048]{1,0:T(8,128)(2,1)} custom-call(bf16[32,32,128]{2,1,0:T(8,128)(2,1)} %attend.1.o_hbm), custom_call_target="tpu_custom_call" | custom-call | tf_op jit(solution)/shard_map/send_back/pallas_call | solution.py:503
  98.6 1.7 %copy.9 = bf16[64,2048]{1,0:T(8,128)(2,1)} copy(bf16[64,2048]{1,0:T(8,128)(2,1)} %send_back.1) | data formatting | bytes 524288

commit v3 on v2

v3 whole, which is shorter than its diff:
```python
import math

import jax
import jax.numpy as jnp
import numpy as np
from jax import lax
from jax.experimental import pallas as pl
from jax.experimental.pallas import tpu as pltpu
from jax.sharding import PartitionSpec as P

MESH = pl.DeviceIdType.MESH
BF16, F32, I32 = jnp.bfloat16, jnp.float32, jnp.int32
WIDTH = 2880
HEAD = 64
BLK = 512
NBLK = 32
SCALE_LOG2 = HEAD**-0.5 * math.log2(math.e)
NEG = -1e30
VMEM = pl.BlockSpec(memory_space=pltpu.VMEM)
HBM = pl.BlockSpec(memory_space=pltpu.HBM)
SMEM = pl.BlockSpec(memory_space=pltpu.SMEM)
OFFSETS = [(dz, dy) for dz in range(8) for dy in range(4) if dz or dy]
INVERSE = (150000.0 ** (-(np.arange(32, dtype=np.float64) * 2.0) / HEAD)).astype(np.float32)


def place():
    z = lax.axis_index("grp")
    s = lax.axis_index("sp")
    return z, s // 8, (s // 2) % 4, s % 2


def dev(z, y, x, c):
    return (z, (y * 4 + x) * 2 + c)


def dot(a, b, ca, cb):
    return lax.dot_general(a, b, (((ca,), (cb,)), ((), ())), preferred_element_type=F32)


class Ring:
    def __init__(self, at, me, right, left, send, recv, first):
        self.at, self.me, self.right, self.left = at, me, right, left
        self.send, self.recv, self.first = send, recv, first
        self.prev, self.next, self.opp = (me + 3) % 4, (me + 1) % 4, (me + 2) % 4

    def copy(self, piece, half, target, k):
        ref = self.at(piece, half)
        return pltpu.make_async_remote_copy(
            src_ref=ref,
            dst_ref=ref,
            send_sem=self.send.at[self.first + k],
            recv_sem=self.recv.at[self.first + k],
            device_id=target,
            device_id_type=MESH,
        )

    def start(self):
        self.copy(self.me, 0, self.right, 0).start()
        self.copy(self.me, 1, self.left, 2).start()
        self.copy(self.me, 1, self.right, 1).start()
        self.copy(self.me, 0, self.left, 3).start()

    def forward(self):
        self.copy(self.prev, 0, self.right, 0).wait_recv()
        self.copy(self.prev, 0, self.right, 4).start()
        self.copy(self.next, 1, self.left, 2).wait_recv()
        self.copy(self.next, 1, self.left, 5).start()

    def near(self):
        self.copy(self.prev, 1, self.right, 1).wait_recv()
        self.copy(self.next, 0, self.left, 3).wait_recv()

    def far(self):
        self.copy(self.opp, 0, self.right, 4).wait_recv()
        self.copy(self.opp, 1, self.left, 5).wait_recv()

    def drain(self):
        self.copy(self.me, 0, self.right, 0).wait_send()
        self.copy(self.me, 1, self.right, 1).wait_send()
        self.copy(self.me, 1, self.left, 2).wait_send()
        self.copy(self.me, 0, self.left, 3).wait_send()
        self.copy(self.prev, 0, self.right, 4).wait_send()
        self.copy(self.next, 1, self.left, 5).wait_send()


def prepare_part(
    places, inv_row, inv_col, tok_hbm, wqt_hbm, kvw_hbm, q_out, kv, order,
    tok, wts, kvw, kvp, stage, angles, lsem, send, recv, zsend, zrecv, psend, precv, qsend, qrecv,
):
    z, y, x, c = place()
    o = 1 - c
    a, b = x * o + y * c, y * o + x * c
    partner = dev(z, y, x, o)
    ring_y = (dev(z, (y + 1) % 4, x, c), dev(z, (y + 3) % 4, x, c))
    ring_x = (dev(z, y, (x + 1) % 4, c), dev(z, y, (x + 3) % 4, c))
    others = [dev((z + d) % 8, y, x, c) for d in range(1, 8)]
    peers = [dev((z + dz) % 8, (y + dy) % 4, x, c) for dz, dy in OFFSETS]
    peers += [*ring_x, partner]

    ready = pltpu.get_barrier_semaphore()
    for peer in peers:
        pl.semaphore_signal(ready, inc=1, device_id=peer, device_id_type=MESH)

    own = [
        pltpu.make_async_copy(tok_hbm, tok.at[y], lsem.at[0]),
        pltpu.make_async_copy(wqt_hbm, wts.at[x, c], lsem.at[1]),
    ]
    for n in range(4):
        cols = pl.ds(256 * n, 256)
        own.append(pltpu.make_async_copy(kvw_hbm.at[:, cols], kvw.at[:, cols], lsem.at[2 + n]))
    for n in (0, 1, 2, 4, 3, 5):
        own[n].start()

    lane = lax.broadcasted_iota(I32, (64, 128), 1)
    base = places[z * 4 + y] * BLK + (x * 2 + c) * 64
    angle = (base + lax.broadcasted_iota(I32, (64, 128), 0)).astype(F32) * inv_row[...]
    cosine = jnp.cos(angle)
    sine = jnp.where(lane % 64 < 32, -1.0, 1.0) * jnp.sin(angle)
    own[0].wait()
    own[1].wait()
    pl.semaphore_wait(ready, len(peers))

    tok_ring = Ring(lambda p, h: tok.at[p, h], y, *ring_y, send, recv, 0)
    wts_ring = Ring(lambda p, h: wts.at[p, c, h], x, *ring_x, send, recv, 6)
    near = [
        dev(z, (y + c) % 4, (x + o) % 4, c),
        dev(z, (y + 3 * c) % 4, (x + 3 * o) % 4, c),
    ]
    wide = [
        dev(z, (y + o) % 4, (x + c) % 4, c),
        dev(z, (y + 3 * o) % 4, (x + 3 * c) % 4, c),
    ]
    kv1_ring = Ring(lambda p, h: kv.at[c, b, p, pl.ds(4 * h, 4)], a, *near, send, recv, 12)
    kv2_ring = Ring(lambda p, h: kv.at[c, p, :, pl.ds(4 * h, 4)], b, *wide, send, recv, 18)

    def with_partner(ref, k):
        return pltpu.make_async_remote_copy(
            src_ref=ref,
            dst_ref=ref,
            send_sem=psend.at[k],
            recv_sem=precv.at[k],
            device_id=partner,
            device_id_type=MESH,
        )

    def exchange(d, head, source):
        return pltpu.make_async_remote_copy(
            src_ref=kvp.at[head],
            dst_ref=kv.at[c, b, a, source],
            send_sem=zsend.at[d - 1],
            recv_sem=zrecv.at[d - 1],
            device_id=others[d - 1],
            device_id_type=MESH,
        )

    tok_ring.start()
    wts_ring.start()
    with_partner(wts.at[x, c], 0).start()

    rows = tok[y].reshape(64, WIDTH)
    for n in range(2):
        own[2 + n].wait()
        own[4 + n].wait()
        keys = jnp.dot(rows, kvw[:, 256 * n : 256 * n + 256], preferred_element_type=F32)
        values = jnp.dot(rows, kvw[:, 512 + 256 * n : 768 + 256 * n], preferred_element_type=F32)
        for p in range(2):
            k, v = keys[:, 128 * p : 128 * p + 128], values[:, 128 * p : 128 * p + 128]
            swapped = jnp.where(lane % 64 < 32, pltpu.roll(k, 96, 1), pltpu.roll(k, 32, 1))
            k = k * cosine + swapped * sine
            kvp[4 * n + 2 * p] = jnp.where(lane < 64, k, pltpu.roll(v, 64, 1)).astype(BF16)
            kvp[4 * n + 2 * p + 1] = jnp.where(lane < 64, pltpu.roll(k, 64, 1), v).astype(BF16)
    kv[c, b, a, z] = kvp[z]

    for d in range(1, 8):
        exchange(d, (z + d) % 8, z).start()

    col = lax.broadcasted_iota(I32, (32, 256), 1)
    block = jnp.where(
        col < 128,
        jnp.where(col < 64, places[z * 4], places[z * 4 + 1]),
        jnp.where(col < 192, places[z * 4 + 2], places[z * 4 + 3]),
    )
    angle = (block * BLK + (x * 2 + c) * 64 + col % 64).astype(F32)
    angle = angle * jnp.concatenate([inv_col[...], inv_col[...]], axis=1)
    angles[0], angles[1] = jnp.cos(angle), jnp.sin(angle)
    def place_block(i, _):
        found = 0
        for n in range(NBLK):
            found = jnp.where(places[n] == i, n, found)
        order[i] = found
        return 0

    lax.fori_loop(0, NBLK, place_block, 0)
    for d in range(1, 8):
        exchange(d, z, (z + 8 - d) % 8).wait_recv()
    kv1_ring.start()

    wts_ring.forward()
    tok_ring.forward()
    wts_ring.near()
    with_partner(wts.at[(x + 3) % 4, c], 1).start()
    with_partner(wts.at[(x + 1) % 4, c], 2).start()
    tok_ring.near()
    kv1_ring.forward()
    wts_ring.far()
    with_partner(wts.at[(x + 2) % 4, c], 3).start()
    kv1_ring.near()
    kv1_ring.far()
    kv2_ring.start()
    with_partner(kv.at[c, b], 4).start()
    tok_ring.far()
    with_partner(wts.at[x, o], 0).wait_recv()
    with_partner(wts.at[(x + 3) % 4, o], 1).wait_recv()
    with_partner(wts.at[(x + 1) % 4, o], 2).wait_recv()
    with_partner(wts.at[(x + 2) % 4, o], 3).wait_recv()

    def message(k):
        return pltpu.make_async_remote_copy(
            src_ref=stage.at[k],
            dst_ref=q_out.at[z],
            send_sem=qsend.at[k],
            recv_sem=qrecv.at[z],
            device_id=dev(2 * y + k // 4, k % 4, x, c),
            device_id_type=MESH,
        )

    def away(k):
        return jnp.logical_or(2 * y + k // 4 != z, k % 4 != y)

    rows = tok[...].reshape(256, WIDTH)
    for half in range(2):
        w = wts[2 * half : 2 * half + 2].reshape(256, WIDTH)
        q = dot(w, rows, 1, 1)
        for i in range(4):
            k = half * 4 + i
            lo, hi = q[i * 64 : i * 64 + 32], q[i * 64 + 32 : i * 64 + 64]
            stage[k, :32] = (lo * angles[0] - hi * angles[1]).astype(BF16)
            stage[k, 32:] = (hi * angles[0] + lo * angles[1]).astype(BF16)
    for k in range(8):

        @pl.when(away(k))
        def _():
            message(k).start()

        @pl.when(jnp.logical_not(away(k)))
        def _():
            q_out[z] = stage[k]

    kv2_ring.forward()
    kv2_ring.near()
    with_partner(kv.at[c, (b + 3) % 4], 5).start()
    with_partner(kv.at[c, (b + 1) % 4], 6).start()
    kv2_ring.far()
    with_partner(kv.at[c, (b + 2) % 4], 7).start()

    for g in range(8):

        @pl.when(jnp.logical_or(g != z, z // 2 != y))
        def _():
            pltpu.make_async_remote_copy(
                src_ref=stage.at[0],
                dst_ref=q_out.at[g],
                send_sem=qsend.at[0],
                recv_sem=qrecv.at[g],
                device_id=dev(g, z // 2, x, c),
                device_id_type=MESH,
            ).wait_recv()

    with_partner(kv.at[o, a], 4).wait_recv()
    with_partner(kv.at[o, (a + 3) % 4], 5).wait_recv()
    with_partner(kv.at[o, (a + 1) % 4], 6).wait_recv()
    with_partner(kv.at[o, (a + 2) % 4], 7).wait_recv()
    for ring in (tok_ring, wts_ring, kv1_ring, kv2_ring):
        ring.drain()
    for d in range(1, 8):
        exchange(d, (z + d) % 8, z).wait_send()
    with_partner(wts.at[x, c], 0).wait_send()
    with_partner(wts.at[(x + 3) % 4, c], 1).wait_send()
    with_partner(wts.at[(x + 1) % 4, c], 2).wait_send()
    with_partner(wts.at[(x + 2) % 4, c], 3).wait_send()
    with_partner(kv.at[c, b], 4).wait_send()
    with_partner(kv.at[c, (b + 3) % 4], 5).wait_send()
    with_partner(kv.at[c, (b + 1) % 4], 6).wait_send()
    with_partner(kv.at[c, (b + 2) % 4], 7).wait_send()
    for k in range(8):

        @pl.when(away(k))
        def _():
            message(k).wait_send()


def attend_part(sinks, q_ref, kv_ref, o_ref, order, vt, qt, gap, s):
    z, y, x, c = place()
    offset = (x * 2 + c) * 64
    sink = sinks[z * 4 + y] * math.log2(math.e)

    key = lax.broadcasted_iota(I32, (BLK, 256), 0)
    col = lax.broadcasted_iota(I32, (BLK, 256), 1)
    key = ((key >> 6) & 3) * 128 + (key >> 8) * 64 + (key & 63)
    gap[...] = key - ((col >> 6) * BLK + offset + (col & 63))

    def keys_of(i):
        b = order[i]
        g, r = b // 4, b % 4
        return kv_ref[0, r, :, g].reshape(256, 128), kv_ref[1, :, r, g].reshape(256, 128)

    lane = lax.broadcasted_iota(I32, (64, 128), 1)
    zero = jnp.where(lax.broadcasted_iota(I32, (80, 256), 0) < 64, 0.0, 1.0)
    vt[...] = jnp.ones((NBLK, 2, 80, 256), BF16)

    def load_queries(first, slot):
        for half in range(2):
            parts = []
            for a in range(2):
                b = order[first + 2 * half + a]
                four = q_ref[b // 4].astype(F32)
                two = jnp.where(b % 4 >= 2, four[:, 128:], four[:, :128])
                parts.append(jnp.where(b % 2 == a, two, pltpu.roll(two, 64, 1)))
            q = jnp.where(lane < 64, *parts)
            qt[slot, :64, 128 * half : 128 * half + 128] = q.astype(BF16)
        qt[slot, 64:] = jnp.zeros((64, 256), BF16)

    def raw_scores(i, slot):
        return [dot(keys, qt[slot], 1, 0) for keys in keys_of(i)]

    def keep(raw, limit, store):
        peaks = []
        for part, scores in enumerate(raw):
            rows = pl.ds(256 * part, 256)
            scores = scores * SCALE_LOG2
            if limit is not None:
                scores = jnp.where(gap[rows] <= limit, scores, NEG)
            store[rows] = scores
            peaks.append(jnp.max(scores, axis=0, keepdims=True))
        return jnp.maximum(*peaks)

    def weigh(i, store, m, acc):
        for part in range(2):
            w = jnp.exp2(store[256 * part : 256 * part + 256] - m).astype(BF16)
            acc = acc + dot(vt[i, part], w, 1, 0)
        return acc

    def step(i, states):
        raw = [raw_scores(i + 1, slot) for slot in range(2)]
        done = []
        for slot in range(2):
            m, acc, peak = states[slot]
            new = jnp.maximum(m, peak)
            acc = weigh(i, s.at[slot], new, acc * jnp.exp2(m - new))
            done.append((new, acc, keep(raw[slot], None, s.at[slot])))
        return tuple(done)

    def finish(first, acc):
        out = acc[:64] / acc[64:65]
        out = jnp.concatenate([out, jnp.zeros((64, 256), F32)], axis=0).T
        for a in range(4):
            top, low = out[64 * a : 64 * a + 32], out[64 * a + 32 : 64 * a + 64]
            o_ref[first + a] = (top + pltpu.roll(low, 64, 1)).astype(BF16)

    def tiles(j, _):
        base = 8 * j
        for slot in range(2):
            load_queries(base + 4 * slot, slot)
        def turn(i):
            for part, keys in enumerate(keys_of(i)):
                vt[i, part, :64] = keys.T[64:]

        def three(u):
            first = jnp.where(u == 4, 0, base + u)
            last = jnp.where(u == 4, 0, base + 4 + u)
            limit = jnp.where(u == 4, 32 * BLK, -u * BLK)
            raw = raw_scores(first, 0), raw_scores(first, 1), raw_scores(last, 1)
            return raw, (limit, None, limit)

        def keep_three(raw, limits):
            return tuple(keep(raw[n], limits[n], s.at[n]) for n in range(3))

        def near(u, carry):
            (m0, acc0), (m1, acc1), (p0, p1, p2) = carry
            raw, limits = three(u + 1)
            turn(base + u)
            turn(base + 4 + u)
            n0 = jnp.maximum(m0, p0)
            n1 = jnp.maximum(m1, jnp.maximum(p1, p2))
            acc0 = weigh(base + u, s.at[0], n0, acc0 * jnp.exp2(m0 - n0))
            acc1 = weigh(base + u, s.at[1], n1, acc1 * jnp.exp2(m1 - n1))
            acc1 = weigh(base + 4 + u, s.at[2], n1, acc1)
            return (n0, acc0), (n1, acc1), keep_three(raw, limits)

        m = jnp.full((1, 256), sink, F32)
        carry = (m, zero), (m, zero), keep_three(*three(0))
        carry = lax.fori_loop(0, 2, lambda t, v: near(2 * t + 1, near(2 * t, v)), carry)
        states = tuple((*carry[slot], carry[2][slot]) for slot in range(2))

        def pair(t, states):
            return step(2 * t + 1, step(2 * t, states))

        states = lax.fori_loop(0, 4 * j, pair, states)
        for slot in range(2):
            finish(base + 4 * slot, states[slot][1])
        return 0

    lax.fori_loop(0, NBLK // 8, tiles, 0)


def return_part(places, o_ref, out, held, own, send, recv):
    z, y, x, c = place()
    for b in range(NBLK):
        own[b] = o_ref[places[b]]
    held[z * 4 + y] = own[z * 4 + y]

    def copy(k, block, head, target):
        return pltpu.make_async_remote_copy(
            src_ref=own.at[block],
            dst_ref=held.at[head],
            send_sem=send.at[k],
            recv_sem=recv.at[k],
            device_id=target,
            device_id_type=MESH,
        )

    def sent(k):
        dz, dy = OFFSETS[k]
        zz, yy = (z + dz) % 8, (y + dy) % 4
        return copy(k, zz * 4 + yy, z * 4 + y, dev(zz, yy, x, c))

    for k in range(31):
        sent(k).start()
    for k, (dz, dy) in enumerate(OFFSETS):
        zz, yy = (z + 8 - dz) % 8, (y + 4 - dy) % 4
        copy(k, 0, zz * 4 + yy, dev(zz, yy, x, c)).wait_recv()
    lane = lax.broadcasted_iota(I32, (32, 128), 1)
    for k in range(16):
        p, q = held[2 * k].astype(F32), held[2 * k + 1].astype(F32)
        cols = pl.ds(128 * k, 128)
        out[:32, cols] = jnp.where(lane < 64, p, pltpu.roll(q, 64, 1)).astype(BF16)
        out[32:, cols] = jnp.where(lane < 64, pltpu.roll(p, 64, 1), q).astype(BF16)
    for k in range(31):
        sent(k).wait_send()


def kernel(
    places, sinks, inv_row, inv_col, tok_hbm, wqt_hbm, kvw_hbm, out,
    q, kv, order, tok, wts, kvw, kvp, stage, angles,
    lsem, send, recv, zsend, zrecv, psend, precv, qsend, qrecv,
    attended, vt, qt, gap, s, held, own, osend, orecv,
):
    prepare_part(
        places, inv_row, inv_col, tok_hbm, wqt_hbm, kvw_hbm, q, kv, order,
        tok, wts, kvw, kvp, stage, angles,
        lsem, send, recv, zsend, zrecv, psend, precv, qsend, qrecv,
    )
    attend_part(sinks, q, kv, attended, order, vt, qt, gap, s)
    return_part(places, attended, out, held, own, osend, orecv)


def per_device(tokens, query_weight, key_value_weight, block_places, sinks):
    dma = pltpu.SemaphoreType.DMA
    return pl.pallas_call(
        kernel,
        in_specs=[SMEM, SMEM, VMEM, VMEM, HBM, HBM, HBM],
        out_specs=VMEM,
        out_shape=jax.ShapeDtypeStruct((64, 2048), BF16),
        scratch_shapes=[
            pltpu.VMEM((8, 64, 256), BF16),
            pltpu.VMEM((2, 4, 4, 8, 64, 128), BF16),
            pltpu.SMEM((NBLK,), I32),
            pltpu.VMEM((4, 2, 32, WIDTH), BF16),
            pltpu.VMEM((4, 2, 2, 32, WIDTH), BF16),
            pltpu.VMEM((WIDTH, 1024), BF16),
            pltpu.VMEM((8, 64, 128), BF16),
            pltpu.VMEM((8, 64, 256), BF16),
            pltpu.VMEM((2, 32, 256), F32),
            dma((6,)),
            dma((24,)),
            dma((24,)),
            dma((7,)),
            dma((7,)),
            dma((8,)),
            dma((8,)),
            dma((8,)),
            dma((8,)),
            pltpu.VMEM((NBLK, 32, 128), BF16),
            pltpu.VMEM((NBLK, 2, 80, 256), BF16),
            pltpu.VMEM((2, 128, 256), BF16),
            pltpu.VMEM((BLK, 256), I32),
            pltpu.VMEM((3, BLK, 256), F32),
            pltpu.VMEM((NBLK, 32, 128), BF16),
            pltpu.VMEM((NBLK, 32, 128), BF16),
            dma((31,)),
            dma((31,)),
        ],
        compiler_params=pltpu.CompilerParams(collective_id=1, has_side_effects=True),
        name="layer",
    )(
        block_places,
        sinks,
        jnp.asarray(np.tile(INVERSE, 4)[None, :]),
        jnp.asarray(np.tile(INVERSE[:, None], (1, 128))),
        tokens.reshape(2, 32, WIDTH),
        query_weight.T.reshape(2, 32, WIDTH),
        key_value_weight,
    )


def solution(mesh):
    in_specs = (P(("grp", "sp"), None), P(None, "sp"), P(), P(), P())
    return jax.shard_map(
        per_device,
        mesh=mesh,
        in_specs=in_specs,
        out_specs=P(("grp", "sp"), None),
        check_vma=False,
    )
```

time: 100 us -> 89.7 us (0.90)
  Pallas kernels: 98.6 us -> 87.8 us
    pallas_call x3 -> x1, Pallas kernels: 98.6 us -> 87.8 us  [per_device(): pl.pallas_call(kernel, in_specs=[SMEM, SMEM, VMEM, VMEM, HBM, HBM, HBM],...]
where the time goes in v3:
time: 89.7 us; the launch traced here: 89.5 us
  Pallas kernels  87.8 us (98%)
  local copies, waits for them, and re-layouts  1.67 us (2%)
    pallas_call x1, Pallas kernels, per_device(): pl.pallas_call(kernel, in_specs=[SMEM, SMEM, VMEM, VMEM, HBM, HBM, HBM],...  87.8 us

profile of v3, /device:TPU:1, one launch (start us, length us, event | category | flops | bytes accessed | tf_op | source)
XLA Modules:
  0.0 89.5 jit_solution(216070124131478256)
XLA Ops:
  0.0 87.8 %layer.1 = bf16[64,2048]{1,0:T(8,128)(2,1)} custom-call(s32[32]{0:T(128)} %places.1, f32[32]{0:T(128)} %sinks.1, f32[1,128]{1,0:T(1,128)} %constant.4.clone.inv_row, f32[32,128]{1,0:T(8,128)} %constant.5.clone.inv_col, bf16[2,32,2880]{2,1,0:T(8,128)(2,1)} %bitcast.4, bf16[2,32,2880]{2,1,0:T(8,128)(2,1)} %bitcast.5, bf16[2880,1024]{1,0:T(8,128)(2,1)} %kvw_hbm.1), custom_call_target="tpu_custom_call" | custom-call | tf_op jit(solution)/shard_map/layer/pallas_call | solution.py:459
  87.8 1.7 %copy.9 = bf16[64,2048]{1,0:T(8,128)(2,1)} copy(bf16[64,2048]{1,0:T(8,128)(2,1)} %layer.1) | data formatting | bytes 524288

commit v4 on v3

--- a/solution.py
+++ b/solution.py
@@ -85,7 +85,7 @@
 
 def prepare_part(
     places, inv_row, inv_col, tok_hbm, wqt_hbm, kvw_hbm, q_out, kv, order,
-    tok, wts, kvw, kvp, stage, angles, lsem, send, recv, zsend, zrecv, psend, precv, qsend, qrecv,
+    tok, wts, kvw, kvp, stage, mid, angles, lsem, send, recv, zsend, zrecv, psend, precv, ysend, yrecv, qsend, qrecv, known,
 ):
     z, y, x, c = place()
     o = 1 - c
@@ -94,8 +94,15 @@
     ring_y = (dev(z, (y + 1) % 4, x, c), dev(z, (y + 3) % 4, x, c))
     ring_x = (dev(z, y, (x + 1) % 4, c), dev(z, y, (x + 3) % 4, c))
     others = [dev((z + d) % 8, y, x, c) for d in range(1, 8)]
-    peers = [dev((z + dz) % 8, (y + dy) % 4, x, c) for dz, dy in OFFSETS]
-    peers += [*ring_x, partner]
+    ring_z = (others[0], others[6])
+    peers = [*ring_y, *ring_x, *ring_z, partner]
+
+    def tell(targets, k):
+        for target in targets:
+            pl.semaphore_signal(known.at[k], inc=1, device_id=target, device_id_type=MESH)
+
+    def hear(targets, k):
+        pl.semaphore_wait(known.at[k], len(targets))
 
     ready = pltpu.get_barrier_semaphore()
     for peer in peers:
@@ -131,7 +138,13 @@
         dev(z, (y + 3 * o) % 4, (x + 3 * c) % 4, c),
     ]
     kv1_ring = Ring(lambda p, h: kv.at[c, b, p, pl.ds(4 * h, 4)], a, *near, send, recv, 12)
-    kv2_ring = Ring(lambda p, h: kv.at[c, p, :, pl.ds(4 * h, 4)], b, *wide, send, recv, 18)
+    kv2_rings = [
+        Ring(
+            lambda p, h, piece=(a + d) % 4: kv.at[c, p, piece, pl.ds(4 * h, 4)],
+            b, *wide, send, recv, 18 + 6 * d,
+        )
+        for d in range(4)
+    ]
 
     def with_partner(ref, k):
         return pltpu.make_async_remote_copy(
@@ -143,6 +156,9 @@
             device_id_type=MESH,
         )
 
+    def piece(n, p):
+        return with_partner(kv.at[c, (b + n) % 4, (a + p) % 4], 4 + 4 * n + p)
+
     def exchange(d, head, source):
         return pltpu.make_async_remote_copy(
             src_ref=kvp.at[head],
@@ -156,6 +172,8 @@
     tok_ring.start()
     wts_ring.start()
     with_partner(wts.at[x, c], 0).start()
+    tell(ring_z, 0)
+    tell(ring_y, 1)
 
     rows = tok[y].reshape(64, WIDTH)
     for n in range(2):
@@ -170,6 +188,13 @@
             kvp[4 * n + 2 * p] = jnp.where(lane < 64, k, pltpu.roll(v, 64, 1)).astype(BF16)
             kvp[4 * n + 2 * p + 1] = jnp.where(lane < 64, pltpu.roll(k, 64, 1), v).astype(BF16)
     kv[c, b, a, z] = kvp[z]
+    hear(ring_z, 0)
+    far_z = (others[1], others[5])
+    tell(far_z, 2)
+    hear(ring_y, 1)
+    hear(far_z, 2)
+    all_y = [dev(z, (y + d) % 4, x, c) for d in (1, 2, 3)]
+    tell(all_y, 3)
 
     for d in range(1, 8):
         exchange(d, (z + d) % 8, z).start()
@@ -194,7 +219,7 @@
     for d in range(1, 8):
         exchange(d, z, (z + 8 - d) % 8).wait_recv()
     kv1_ring.start()
-
+    kv2_rings[0].start()
     wts_ring.forward()
     tok_ring.forward()
     wts_ring.near()
@@ -202,91 +227,123 @@
     with_partner(wts.at[(x + 1) % 4, c], 2).start()
     tok_ring.near()
     kv1_ring.forward()
+    kv2_rings[0].forward()
+    kv1_ring.near()
+    kv2_rings[1].start()
+    kv2_rings[3].start()
     wts_ring.far()
     with_partner(wts.at[(x + 2) % 4, c], 3).start()
-    kv1_ring.near()
-    kv1_ring.far()
-    kv2_ring.start()
-    with_partner(kv.at[c, b], 4).start()
     tok_ring.far()
     with_partner(wts.at[x, o], 0).wait_recv()
     with_partner(wts.at[(x + 3) % 4, o], 1).wait_recv()
     with_partner(wts.at[(x + 1) % 4, o], 2).wait_recv()
     with_partner(wts.at[(x + 2) % 4, o], 3).wait_recv()
 
-    def message(k):
+    hear(all_y, 3)
+    def along_y(d, half, target, source):
         return pltpu.make_async_remote_copy(
-            src_ref=stage.at[k],
+            src_ref=stage.at[target, half],
+            dst_ref=mid.at[2 * source + half],
+            send_sem=ysend.at[2 * d + half],
+            recv_sem=yrecv.at[2 * d + half],
+            device_id=dev(z, (y + d) % 4, x, c),
+            device_id_type=MESH,
+        )
+
+    def along_z(d, half):
+        plane = 2 * ((y + 4 - d) % 4) + half
+        return plane, pltpu.make_async_remote_copy(
+            src_ref=mid.at[plane],
             dst_ref=q_out.at[z],
-            send_sem=qsend.at[k],
+            send_sem=qsend.at[2 * d + half],
             recv_sem=qrecv.at[z],
-            device_id=dev(2 * y + k // 4, k % 4, x, c),
+            device_id=dev(plane, y, x, c),
             device_id_type=MESH,
         )
 
-    def away(k):
-        return jnp.logical_or(2 * y + k // 4 != z, k % 4 != y)
+    def pass_on(d, half):
+        plane, copy = along_z(d, half)
+
+        @pl.when(plane != z)
+        def _():
+            copy.start()
+
+        @pl.when(plane == z)
+        def _():
+            q_out[z] = mid[plane]
 
     rows = tok[...].reshape(256, WIDTH)
     for half in range(2):
         w = wts[2 * half : 2 * half + 2].reshape(256, WIDTH)
         q = dot(w, rows, 1, 1)
         for i in range(4):
-            k = half * 4 + i
             lo, hi = q[i * 64 : i * 64 + 32], q[i * 64 + 32 : i * 64 + 64]
-            stage[k, :32] = (lo * angles[0] - hi * angles[1]).astype(BF16)
-            stage[k, 32:] = (hi * angles[0] + lo * angles[1]).astype(BF16)
-    for k in range(8):
-
-        @pl.when(away(k))
-        def _():
-            message(k).start()
-
-        @pl.when(jnp.logical_not(away(k)))
-        def _():
-            q_out[z] = stage[k]
-
-    kv2_ring.forward()
-    kv2_ring.near()
-    with_partner(kv.at[c, (b + 3) % 4], 5).start()
-    with_partner(kv.at[c, (b + 1) % 4], 6).start()
-    kv2_ring.far()
-    with_partner(kv.at[c, (b + 2) % 4], 7).start()
+            stage[i, half, :32] = (lo * angles[0] - hi * angles[1]).astype(BF16)
+            stage[i, half, 32:] = (hi * angles[0] + lo * angles[1]).astype(BF16)
+        for d in (2, 1, 3):
+            along_y(d, half, (y + d) % 4, y).start()
+        mid[2 * y + half] = stage[y, half]
+    for half in range(2):
+        pass_on(0, half)
+
+    kv1_ring.far()
+    kv2_rings[2].start()
+    for p in range(4):
+        piece(0, p).start()
+    kv2_rings[1].forward()
+    kv2_rings[3].forward()
+
+    for half in range(2):
+        for d in (1, 3, 2):
+            along_y(d, half, y, (y + 4 - d) % 4).wait_recv()
+            pass_on(d, half)
+
+    kv2_rings[2].forward()
+    for p in (0, 1, 3, 2):
+        kv2_rings[p].near()
+        piece(1, p).start()
+        piece(3, p).start()
+    for p in (0, 1, 3, 2):
+        kv2_rings[p].far()
+        piece(2, p).start()
 
     for g in range(8):
 
-        @pl.when(jnp.logical_or(g != z, z // 2 != y))
+        @pl.when(g != z)
         def _():
             pltpu.make_async_remote_copy(
-                src_ref=stage.at[0],
+                src_ref=mid.at[0],
                 dst_ref=q_out.at[g],
                 send_sem=qsend.at[0],
                 recv_sem=qrecv.at[g],
-                device_id=dev(g, z // 2, x, c),
+                device_id=dev(g, y, x, c),
                 device_id_type=MESH,
             ).wait_recv()
 
-    with_partner(kv.at[o, a], 4).wait_recv()
-    with_partner(kv.at[o, (a + 3) % 4], 5).wait_recv()
-    with_partner(kv.at[o, (a + 1) % 4], 6).wait_recv()
-    with_partner(kv.at[o, (a + 2) % 4], 7).wait_recv()
-    for ring in (tok_ring, wts_ring, kv1_ring, kv2_ring):
+    for n in range(4):
+        for p in range(4):
+            with_partner(kv.at[o, (a + n) % 4, (b + p) % 4], 4 + 4 * n + p).wait_recv()
+    for ring in (tok_ring, wts_ring, kv1_ring, *kv2_rings):
         ring.drain()
     for d in range(1, 8):
         exchange(d, (z + d) % 8, z).wait_send()
+    for half in range(2):
+        for d in range(1, 4):
+            along_y(d, half, (y + d) % 4, y).wait_send()
+        for d in range(4):
+            plane, copy = along_z(d, half)
+
+            @pl.when(plane != z)
+            def _():
+                copy.wait_send()
+
     with_partner(wts.at[x, c], 0).wait_send()
     with_partner(wts.at[(x + 3) % 4, c], 1).wait_send()
     with_partner(wts.at[(x + 1) % 4, c], 2).wait_send()
     with_partner(wts.at[(x + 2) % 4, c], 3).wait_send()
-    with_partner(kv.at[c, b], 4).wait_send()
-    with_partner(kv.at[c, (b + 3) % 4], 5).wait_send()
-    with_partner(kv.at[c, (b + 1) % 4], 6).wait_send()
-    with_partner(kv.at[c, (b + 2) % 4], 7).wait_send()
-    for k in range(8):
-
-        @pl.when(away(k))
-        def _():
-            message(k).wait_send()
+    for n in range(4):
+        for p in range(4):
+            piece(n, p).wait_send()
 
 
 def attend_part(sinks, q_ref, kv_ref, o_ref, order, vt, qt, gap, s):
@@ -392,10 +449,12 @@
         carry = lax.fori_loop(0, 2, lambda t, v: near(2 * t + 1, near(2 * t, v)), carry)
         states = tuple((*carry[slot], carry[2][slot]) for slot in range(2))
 
-        def pair(t, states):
-            return step(2 * t + 1, step(2 * t, states))
-
-        states = lax.fori_loop(0, 4 * j, pair, states)
+        def four(t, states):
+            for n in range(4):
+                states = step(4 * t + n, states)
+            return states
+
+        states = lax.fori_loop(0, 2 * j, four, states)
         for slot in range(2):
             finish(base + 4 * slot, states[slot][1])
         return 0
@@ -441,14 +500,14 @@
 
 def kernel(
     places, sinks, inv_row, inv_col, tok_hbm, wqt_hbm, kvw_hbm, out,
-    q, kv, order, tok, wts, kvw, kvp, stage, angles,
-    lsem, send, recv, zsend, zrecv, psend, precv, qsend, qrecv,
+    q, kv, order, tok, wts, kvw, kvp, stage, mid, angles,
+    lsem, send, recv, zsend, zrecv, psend, precv, ysend, yrecv, qsend, qrecv, known,
     attended, vt, qt, gap, s, held, own, osend, orecv,
 ):
     prepare_part(
         places, inv_row, inv_col, tok_hbm, wqt_hbm, kvw_hbm, q, kv, order,
-        tok, wts, kvw, kvp, stage, angles,
-        lsem, send, recv, zsend, zrecv, psend, precv, qsend, qrecv,
+        tok, wts, kvw, kvp, stage, mid, angles,
+        lsem, send, recv, zsend, zrecv, psend, precv, ysend, yrecv, qsend, qrecv, known,
     )
     attend_part(sinks, q, kv, attended, order, vt, qt, gap, s)
     return_part(places, attended, out, held, own, osend, orecv)
@@ -469,17 +528,21 @@
             pltpu.VMEM((4, 2, 2, 32, WIDTH), BF16),
             pltpu.VMEM((WIDTH, 1024), BF16),
             pltpu.VMEM((8, 64, 128), BF16),
+            pltpu.VMEM((4, 2, 64, 256), BF16),
             pltpu.VMEM((8, 64, 256), BF16),
             pltpu.VMEM((2, 32, 256), F32),
             dma((6,)),
-            dma((24,)),
-            dma((24,)),
+            dma((42,)),
+            dma((42,)),
             dma((7,)),
             dma((7,)),
+            dma((20,)),
+            dma((20,)),
             dma((8,)),
             dma((8,)),
             dma((8,)),
             dma((8,)),
+            pltpu.SemaphoreType.REGULAR((4,)),
             pltpu.VMEM((NBLK, 32, 128), BF16),
             pltpu.VMEM((NBLK, 2, 80, 256), BF16),
             pltpu.VMEM((2, 128, 256), BF16),

time: 89.7 us -> 80.9 us (0.902)
  Pallas kernels: 87.8 us -> 79 us
    pallas_call x1, Pallas kernels: 87.8 us -> 79 us  [per_device(): pl.pallas_call(kernel, in_specs=[SMEM, SMEM, VMEM, VMEM, HBM, HBM, HBM],...]
where the time goes in v4:
time: 80.9 us; the launch traced here: 80.7 us
  Pallas kernels  79 us (98%)
  local copies, waits for them, and re-layouts  1.67 us (2%)
    pallas_call x1, Pallas kernels, per_device(): pl.pallas_call(kernel, in_specs=[SMEM, SMEM, VMEM, VMEM, HBM, HBM, HBM],...  79 us
    unnamed x1, local copies, waits for them, and re-layouts  1.67 us

profile of v4, /device:TPU:1, one launch (start us, length us, event | category | flops | bytes accessed | tf_op | source)
XLA Modules:
  0.0 80.7 jit_solution(15945885470599783714)
XLA Ops:
  0.0 79.0 %layer.1 = bf16[64,2048]{1,0:T(8,128)(2,1)} custom-call(s32[32]{0:T(128)} %places.1, f32[32]{0:T(128)} %sinks.1, f32[1,128]{1,0:T(1,128)} %constant.4.clone.inv_row, f32[32,128]{1,0:T(8,128)} %constant.5.clone.inv_col, bf16[2,32,2880]{2,1,0:T(8,128)(2,1)} %bitcast.4, bf16[2,32,2880]{2,1,0:T(8,128)(2,1)} %bitcast.5, bf16[2880,1024]{1,0:T(8,128)(2,1)} %kvw_hbm.1), custom_call_target="tpu_custom_call" | custom-call | tf_op jit(solution)/shard_map/layer/pallas_call | solution.py:518
  79.0 1.7 %copy.9 = bf16[64,2048]{1,0:T(8,128)(2,1)} copy(bf16[64,2048]{1,0:T(8,128)(2,1)} %layer.1) | data formatting | bytes 524288

commit v5 on v4

--- a/solution.py
+++ b/solution.py
@@ -20,6 +20,7 @@
 HBM = pl.BlockSpec(memory_space=pltpu.HBM)
 SMEM = pl.BlockSpec(memory_space=pltpu.SMEM)
 OFFSETS = [(dz, dy) for dz in range(8) for dy in range(4) if dz or dy]
+OFFSETS.sort(key=lambda o: -(min(o[0], 8 - o[0]) + min(o[1], 4 - o[1])))
 INVERSE = (150000.0 ** (-(np.arange(32, dtype=np.float64) * 2.0) / HEAD)).astype(np.float32)
 
 
@@ -84,7 +85,7 @@
 
 
 def prepare_part(
-    places, inv_row, inv_col, tok_hbm, wqt_hbm, kvw_hbm, q_out, kv, order,
+    idle, queries_here, small, places, inv_row, inv_col, tok_hbm, wqt_hbm, kvw_hbm, q_out, kv, order,
     tok, wts, kvw, kvp, stage, mid, angles, lsem, send, recv, zsend, zrecv, psend, precv, ysend, yrecv, qsend, qrecv, known,
 ):
     z, y, x, c = place()
@@ -115,9 +116,15 @@
     for n in range(4):
         cols = pl.ds(256 * n, 256)
         own.append(pltpu.make_async_copy(kvw_hbm.at[:, cols], kvw.at[:, cols], lsem.at[2 + n]))
-    for n in (0, 1, 2, 4, 3, 5):
+    for n in (0, 1):
         own[n].start()
-
+    for copy in small:
+        copy.start()
+    for n in (2, 4, 3, 5):
+        own[n].start()
+
+    for copy in small:
+        copy.wait()
     lane = lax.broadcasted_iota(I32, (64, 128), 1)
     base = places[z * 4 + y] * BLK + (x * 2 + c) * 64
     angle = (base + lax.broadcasted_iota(I32, (64, 128), 0)).astype(F32) * inv_row[...]
@@ -196,7 +203,7 @@
     all_y = [dev(z, (y + d) % 4, x, c) for d in (1, 2, 3)]
     tell(all_y, 3)
 
-    for d in range(1, 8):
+    for d in (4, 3, 5, 2, 6, 1, 7):
         exchange(d, (z + d) % 8, z).start()
 
     col = lax.broadcasted_iota(I32, (32, 256), 1)
@@ -216,6 +223,7 @@
         return 0
 
     lax.fori_loop(0, NBLK, place_block, 0)
+    idle()
     for d in range(1, 8):
         exchange(d, z, (z + 8 - d) % 8).wait_recv()
     kv1_ring.start()
@@ -320,6 +328,7 @@
                 device_id_type=MESH,
             ).wait_recv()
 
+    queries_here()
     for n in range(4):
         for p in range(4):
             with_partner(kv.at[o, (a + n) % 4, (b + p) % 4], 4 + 4 * n + p).wait_recv()
@@ -346,39 +355,48 @@
             piece(n, p).wait_send()
 
 
-def attend_part(sinks, q_ref, kv_ref, o_ref, order, vt, qt, gap, s):
+def attend_tables(vt, gap):
     z, y, x, c = place()
     offset = (x * 2 + c) * 64
-    sink = sinks[z * 4 + y] * math.log2(math.e)
-
     key = lax.broadcasted_iota(I32, (BLK, 256), 0)
     col = lax.broadcasted_iota(I32, (BLK, 256), 1)
     key = ((key >> 6) & 3) * 128 + (key >> 8) * 64 + (key & 63)
     gap[...] = key - ((col >> 6) * BLK + offset + (col & 63))
+    vt[...] = jnp.ones((NBLK, 2, 80, 256), BF16)
+
+
+def attend_queries(q_ref, order, qt):
+    lane = lax.broadcasted_iota(I32, (64, 128), 1)
+
+    def load_queries(tile, _):
+        for half in range(2):
+            parts = []
+            for a in range(2):
+                b = order[4 * tile + 2 * half + a]
+                four = q_ref[b // 4].astype(F32)
+                two = jnp.where(b % 4 >= 2, four[:, 128:], four[:, :128])
+                parts.append(jnp.where(b % 2 == a, two, pltpu.roll(two, 64, 1)))
+            q = jnp.where(lane < 64, *parts)
+            qt[tile, :64, 128 * half : 128 * half + 128] = q.astype(BF16)
+        qt[tile, 64:] = jnp.zeros((64, 256), BF16)
+        return 0
+
+    lax.fori_loop(0, 8, load_queries, 0, unroll=4)
+
+
+def attend_part(sinks, kv_ref, o_ref, order, vt, qt, gap, s):
+    z, y, x, c = place()
+    sink = sinks[z * 4 + y] * math.log2(math.e)
 
     def keys_of(i):
         b = order[i]
         g, r = b // 4, b % 4
         return kv_ref[0, r, :, g].reshape(256, 128), kv_ref[1, :, r, g].reshape(256, 128)
 
-    lane = lax.broadcasted_iota(I32, (64, 128), 1)
     zero = jnp.where(lax.broadcasted_iota(I32, (80, 256), 0) < 64, 0.0, 1.0)
-    vt[...] = jnp.ones((NBLK, 2, 80, 256), BF16)
-
-    def load_queries(first, slot):
-        for half in range(2):
-            parts = []
-            for a in range(2):
-                b = order[first + 2 * half + a]
-                four = q_ref[b // 4].astype(F32)
-                two = jnp.where(b % 4 >= 2, four[:, 128:], four[:, :128])
-                parts.append(jnp.where(b % 2 == a, two, pltpu.roll(two, 64, 1)))
-            q = jnp.where(lane < 64, *parts)
-            qt[slot, :64, 128 * half : 128 * half + 128] = q.astype(BF16)
-        qt[slot, 64:] = jnp.zeros((64, 256), BF16)
-
-    def raw_scores(i, slot):
-        return [dot(keys, qt[slot], 1, 0) for keys in keys_of(i)]
+
+    def raw_scores(i, tile):
+        return [dot(keys, qt[tile], 1, 0) for keys in keys_of(i)]
 
     def keep(raw, limit, store):
         peaks = []
@@ -397,16 +415,6 @@
             acc = acc + dot(vt[i, part], w, 1, 0)
         return acc
 
-    def step(i, states):
-        raw = [raw_scores(i + 1, slot) for slot in range(2)]
-        done = []
-        for slot in range(2):
-            m, acc, peak = states[slot]
-            new = jnp.maximum(m, peak)
-            acc = weigh(i, s.at[slot], new, acc * jnp.exp2(m - new))
-            done.append((new, acc, keep(raw[slot], None, s.at[slot])))
-        return tuple(done)
-
     def finish(first, acc):
         out = acc[:64] / acc[64:65]
         out = jnp.concatenate([out, jnp.zeros((64, 256), F32)], axis=0).T
@@ -414,27 +422,42 @@
             top, low = out[64 * a : 64 * a + 32], out[64 * a + 32 : 64 * a + 64]
             o_ref[first + a] = (top + pltpu.roll(low, 64, 1)).astype(BF16)
 
-    def tiles(j, _):
+    def turn(i):
+        for part, keys in enumerate(keys_of(i)):
+            vt[i, part, :64] = keys.T[64:]
+
+    def three(j, u):
+        raw = (
+            raw_scores(8 * j + u, 2 * j),
+            raw_scores(8 * j + u, 2 * j + 1),
+            raw_scores(8 * j + 4 + u, 2 * j + 1),
+        )
+        return raw, (-u * BLK, None, -u * BLK)
+
+    def keep_three(raw, limits):
+        return tuple(keep(raw[n], limits[n], s.at[n]) for n in range(3))
+
+    def tiles(j, peaks):
         base = 8 * j
-        for slot in range(2):
-            load_queries(base + 4 * slot, slot)
-        def turn(i):
-            for part, keys in enumerate(keys_of(i)):
-                vt[i, part, :64] = keys.T[64:]
-
-        def three(u):
-            first = jnp.where(u == 4, 0, base + u)
-            last = jnp.where(u == 4, 0, base + 4 + u)
-            limit = jnp.where(u == 4, 32 * BLK, -u * BLK)
-            raw = raw_scores(first, 0), raw_scores(first, 1), raw_scores(last, 1)
-            return raw, (limit, None, limit)
-
-        def keep_three(raw, limits):
-            return tuple(keep(raw[n], limits[n], s.at[n]) for n in range(3))
-
-        def near(u, carry):
+
+        def step(i, states):
+            raw = [raw_scores(i + 1, 2 * j + slot) for slot in range(2)]
+            done = []
+            for slot in range(2):
+                m, acc, peak = states[slot]
+                new = jnp.maximum(m, peak)
+                acc = weigh(i, s.at[slot], new, acc * jnp.exp2(m - new))
+                done.append((new, acc, keep(raw[slot], None, s.at[slot])))
+            return tuple(done)
+
+        m = jnp.full((1, 256), sink, F32)
+        carry = (m, zero), (m, zero), peaks
+        for u in range(4):
             (m0, acc0), (m1, acc1), (p0, p1, p2) = carry
-            raw, limits = three(u + 1)
+            if u < 3:
+                raw, limits = three(j, u + 1)
+            else:
+                raw = [raw_scores(0, 2 * j), raw_scores(0, 2 * j + 1)]
             turn(base + u)
             turn(base + 4 + u)
             n0 = jnp.maximum(m0, p0)
@@ -442,24 +465,25 @@
             acc0 = weigh(base + u, s.at[0], n0, acc0 * jnp.exp2(m0 - n0))
             acc1 = weigh(base + u, s.at[1], n1, acc1 * jnp.exp2(m1 - n1))
             acc1 = weigh(base + 4 + u, s.at[2], n1, acc1)
-            return (n0, acc0), (n1, acc1), keep_three(raw, limits)
-
-        m = jnp.full((1, 256), sink, F32)
-        carry = (m, zero), (m, zero), keep_three(*three(0))
-        carry = lax.fori_loop(0, 2, lambda t, v: near(2 * t + 1, near(2 * t, v)), carry)
+            if u < 3:
+                peaks = keep_three(raw, limits)
+            else:
+                peaks = [keep(raw[n], None, s.at[n]) for n in range(2)]
+            carry = (n0, acc0), (n1, acc1), peaks
         states = tuple((*carry[slot], carry[2][slot]) for slot in range(2))
 
-        def four(t, states):
-            for n in range(4):
-                states = step(4 * t + n, states)
+        def eight(t, states):
+            for n in range(8):
+                states = step(8 * t + n, states)
             return states
 
-        states = lax.fori_loop(0, 2 * j, four, states)
+        states = lax.fori_loop(0, j, eight, states)
+        peaks = keep_three(*three(jnp.minimum(j + 1, 3), 0))
         for slot in range(2):
             finish(base + 4 * slot, states[slot][1])
-        return 0
-
-    lax.fori_loop(0, NBLK // 8, tiles, 0)
+        return peaks
+
+    lax.fori_loop(0, NBLK // 8, tiles, keep_three(*three(0, 0)))
 
 
 def return_part(places, o_ref, out, held, own, send, recv):
@@ -499,17 +523,25 @@
 
 
 def kernel(
-    places, sinks, inv_row, inv_col, tok_hbm, wqt_hbm, kvw_hbm, out,
+    places_hbm, sinks_hbm, row_hbm, col_hbm, tok_hbm, wqt_hbm, kvw_hbm, out,
+    places, sinks, inv_row, inv_col, ssem,
     q, kv, order, tok, wts, kvw, kvp, stage, mid, angles,
     lsem, send, recv, zsend, zrecv, psend, precv, ysend, yrecv, qsend, qrecv, known,
     attended, vt, qt, gap, s, held, own, osend, orecv,
 ):
+    small = [
+        pltpu.make_async_copy(places_hbm, places, ssem.at[0]),
+        pltpu.make_async_copy(sinks_hbm, sinks, ssem.at[1]),
+        pltpu.make_async_copy(row_hbm, inv_row, ssem.at[2]),
+        pltpu.make_async_copy(col_hbm, inv_col, ssem.at[3]),
+    ]
     prepare_part(
-        places, inv_row, inv_col, tok_hbm, wqt_hbm, kvw_hbm, q, kv, order,
+        lambda: attend_tables(vt, gap), lambda: attend_queries(q, order, qt),
+        small, places, inv_row, inv_col, tok_hbm, wqt_hbm, kvw_hbm, q, kv, order,
         tok, wts, kvw, kvp, stage, mid, angles,
         lsem, send, recv, zsend, zrecv, psend, precv, ysend, yrecv, qsend, qrecv, known,
     )
-    attend_part(sinks, q, kv, attended, order, vt, qt, gap, s)
+    attend_part(sinks, kv, attended, order, vt, qt, gap, s)
     return_part(places, attended, out, held, own, osend, orecv)
 
 
@@ -517,10 +549,15 @@
     dma = pltpu.SemaphoreType.DMA
     return pl.pallas_call(
         kernel,
-        in_specs=[SMEM, SMEM, VMEM, VMEM, HBM, HBM, HBM],
+        in_specs=[HBM] * 7,
         out_specs=VMEM,
         out_shape=jax.ShapeDtypeStruct((64, 2048), BF16),
         scratch_shapes=[
+            pltpu.SMEM((NBLK,), I32),
+            pltpu.SMEM((32,), F32),
+            pltpu.VMEM((1, 128), F32),
+            pltpu.VMEM((32, 128), F32),
+            dma((4,)),
             pltpu.VMEM((8, 64, 256), BF16),
             pltpu.VMEM((2, 4, 4, 8, 64, 128), BF16),
             pltpu.SMEM((NBLK,), I32),
@@ -545,7 +582,7 @@
             pltpu.SemaphoreType.REGULAR((4,)),
             pltpu.VMEM((NBLK, 32, 128), BF16),
             pltpu.VMEM((NBLK, 2, 80, 256), BF16),
-            pltpu.VMEM((2, 128, 256), BF16),
+            pltpu.VMEM((8, 128, 256), BF16),
             pltpu.VMEM((BLK, 256), I32),
             pltpu.VMEM((3, BLK, 256), F32),
             pltpu.VMEM((NBLK, 32, 128), BF16),

time: 80.9 us -> 76.5 us (0.946)
  Pallas kernels: 79 us -> 74.8 us
    pallas_call x1, Pallas kernels: 79 us -> 74.8 us  [per_device(): pl.pallas_call(kernel, in_specs=[HBM] * 7, out_specs=VMEM, out_shape=jax....]
where the time goes in v5:
time: 76.5 us; the launch traced here: 76.4 us
  Pallas kernels  74.8 us (98%)
  local copies, waits for them, and re-layouts  1.67 us (2%)
    pallas_call x1, Pallas kernels, per_device(): pl.pallas_call(kernel, in_specs=[HBM] * 7, out_specs=VMEM, out_shape=jax....  74.8 us
    unnamed x1, local copies, waits for them, and re-layouts  1.67 us

profile of v5, /device:TPU:1, one launch (start us, length us, event | category | flops | bytes accessed | tf_op | source)
XLA Modules:
  0.0 76.4 jit_solution(16879814148785097740)
XLA Ops:
  0.0 74.8 %layer.1 = bf16[64,2048]{1,0:T(8,128)(2,1)} custom-call(s32[32]{0:T(128)} %places_hbm.1, f32[32]{0:T(128)} %sinks_hbm.1, f32[1,128]{1,0:T(1,128)} %constant.4.clone.row_hbm, f32[32,128]{1,0:T(8,128)} %constant.5.clone.col_hbm, bf16[2,32,2880]{2,1,0:T(8,128)(2,1)} %bitcast.4, bf16[2,32,2880]{2,1,0:T(8,128)(2,1)} %bitcast.5, bf16[2880,1024]{1,0:T(8,128)(2,1)} %kvw_hbm.1), custom_call_target="tpu_custom_call" | custom-call | tf_op jit(solution)/shard_map/layer/pallas_call | solution.py:550
  74.8 1.7 %copy.9 = bf16[64,2048]{1,0:T(8,128)(2,1)} copy(bf16[64,2048]{1,0:T(8,128)(2,1)} %layer.1) | data formatting | bytes 524288

commit v6 on v5

--- a/solution.py
+++ b/solution.py
@@ -206,6 +206,10 @@
     for d in (4, 3, 5, 2, 6, 1, 7):
         exchange(d, (z + d) % 8, z).start()
 
+    for d in range(1, 8):
+        exchange(d, z, (z + 8 - d) % 8).wait_recv()
+    kv1_ring.start()
+    kv2_rings[0].start()
     col = lax.broadcasted_iota(I32, (32, 256), 1)
     block = jnp.where(
         col < 128,
@@ -215,19 +219,6 @@
     angle = (block * BLK + (x * 2 + c) * 64 + col % 64).astype(F32)
     angle = angle * jnp.concatenate([inv_col[...], inv_col[...]], axis=1)
     angles[0], angles[1] = jnp.cos(angle), jnp.sin(angle)
-    def place_block(i, _):
-        found = 0
-        for n in range(NBLK):
-            found = jnp.where(places[n] == i, n, found)
-        order[i] = found
-        return 0
-
-    lax.fori_loop(0, NBLK, place_block, 0)
-    idle()
-    for d in range(1, 8):
-        exchange(d, z, (z + 8 - d) % 8).wait_recv()
-    kv1_ring.start()
-    kv2_rings[0].start()
     wts_ring.forward()
     tok_ring.forward()
     wts_ring.near()
@@ -307,6 +298,15 @@
             pass_on(d, half)
 
     kv2_rings[2].forward()
+    def place_block(i, _):
+        found = 0
+        for n in range(NBLK):
+            found = jnp.where(places[n] == i, n, found)
+        order[i] = found
+        return 0
+
+    lax.fori_loop(0, NBLK, place_block, 0)
+    idle()
     for p in (0, 1, 3, 2):
         kv2_rings[p].near()
         piece(1, p).start()
@@ -456,7 +456,7 @@
             (m0, acc0), (m1, acc1), (p0, p1, p2) = carry
             if u < 3:
                 raw, limits = three(j, u + 1)
-            else:
+            elif j:
                 raw = [raw_scores(0, 2 * j), raw_scores(0, 2 * j + 1)]
             turn(base + u)
             turn(base + 4 + u)
@@ -467,7 +467,7 @@
             acc1 = weigh(base + 4 + u, s.at[2], n1, acc1)
             if u < 3:
                 peaks = keep_three(raw, limits)
-            else:
+            elif j:
                 peaks = [keep(raw[n], None, s.at[n]) for n in range(2)]
             carry = (n0, acc0), (n1, acc1), peaks
         states = tuple((*carry[slot], carry[2][slot]) for slot in range(2))
@@ -477,13 +477,17 @@
                 states = step(8 * t + n, states)
             return states
 
-        states = lax.fori_loop(0, j, eight, states)
-        peaks = keep_three(*three(jnp.minimum(j + 1, 3), 0))
+        if j:
+            states = lax.fori_loop(0, j, eight, states)
+        if j < 3:
+            peaks = keep_three(*three(j + 1, 0))
         for slot in range(2):
             finish(base + 4 * slot, states[slot][1])
         return peaks
 
-    lax.fori_loop(0, NBLK // 8, tiles, keep_three(*three(0, 0)))
+    peaks = keep_three(*three(0, 0))
+    for j in range(NBLK // 8):
+        peaks = tiles(j, peaks)
 
 
 def return_part(places, o_ref, out, held, own, send, recv):

time: 76.5 us -> 75.3 us (0.984)
  Pallas kernels: 74.8 us -> 73.5 us
    pallas_call x1, Pallas kernels: 74.8 us -> 73.5 us  [per_device(): pl.pallas_call(kernel, in_specs=[HBM] * 7, out_specs=VMEM, out_shape=jax....]
where the time goes in v6:
time: 75.3 us; the launch traced here: 75.2 us
  Pallas kernels  73.5 us (98%)
  local copies, waits for them, and re-layouts  1.67 us (2%)
    pallas_call x1, Pallas kernels, per_device(): pl.pallas_call(kernel, in_specs=[HBM] * 7, out_specs=VMEM, out_shape=jax....  73.5 us
    unnamed x1, local copies, waits for them, and re-layouts  1.67 us

profile of v6, /device:TPU:1, one launch (start us, length us, event | category | flops | bytes accessed | tf_op | source)
XLA Modules:
  0.0 75.2 jit_solution(5168993985678209985)
XLA Ops:
  0.0 73.5 %layer.1 = bf16[64,2048]{1,0:T(8,128)(2,1)} custom-call(s32[32]{0:T(128)} %places_hbm.1, f32[32]{0:T(128)} %sinks_hbm.1, f32[1,128]{1,0:T(1,128)} %constant.4.clone.row_hbm, f32[32,128]{1,0:T(8,128)} %constant.5.clone.col_hbm, bf16[2,32,2880]{2,1,0:T(8,128)(2,1)} %bitcast.4, bf16[2,32,2880]{2,1,0:T(8,128)(2,1)} %bitcast.5, bf16[2880,1024]{1,0:T(8,128)(2,1)} %kvw_hbm.1), custom_call_target="tpu_custom_call" | custom-call | tf_op jit(solution)/shard_map/layer/pallas_call | solution.py:554
  73.5 1.7 %copy.9 = bf16[64,2048]{1,0:T(8,128)(2,1)} copy(bf16[64,2048]{1,0:T(8,128)(2,1)} %layer.1) | data formatting | bytes 524288
